TPU v7x, 512 devices: a whole 4x8x8 slice. The times are simulated.
512 devices in a mesh: sp: 64 (over z, y_hi, x), tp: 8 (over y_lo, core).
Axes of the slice: x: 4, y: 8 (y_hi: 2, y_lo: 4; y = y_hi * 4 + y_lo), z: 8, core: 2. Of those that a mesh axis runs over, the one named last changes fastest.
Arguments:
- fade_rate: float32 [1, 65536, 4096], P(None, 'sp', 'tp'), may hold values from 0.2 to 2
- update_in: bfloat16 [1, 65536, 4096], P(None, 'sp', 'tp'), may hold values from -6 to 6
- norm_gain: float32 [4096], P('tp'), may hold values from 0.25 to 1.75
Outputs:
- mixed_out: bfloat16 [1, 65536, 4096], P(None, 'sp', 'tp')
All inputs are finite; a program needn't handle non-finite values.
Results may differ from a plain program's by a relative error of at most 0.0011.
Values sent between devices are 32-bit elements; how exact they have to be, the bound alone decides.
No kernel may reach another device: no remote copies, remote signals or barrier semaphores. Data moves between devices by JAX's collectives and lax.ppermute only.
A program may use at most 64 MiB of HBM per device.

v0:
```python
import jax
import jax.numpy as jnp
from jax import lax
from jax.sharding import PartitionSpec as P


def copy_for_each(shard, axis):
    copies = jnp.broadcast_to(shard, (lax.axis_size(axis), *shard.shape))
    return lax.all_to_all(copies, axis, split_axis=0, concat_axis=0, tiled=True)


def all_in_one(shard, axis):
    leaves = jax.tree.leaves(shard)
    sequence = sorted(range(len(leaves)), key=lambda k: -leaves[k].size)
    width = (1, *leaves[sequence[0]].shape)[-1]
    lines = [
        jnp.pad(leaves[k].reshape(-1), (0, -leaves[k].size % width)).reshape(-1, width)
        for k in sequence
    ]
    both, at, found = (copy_for_each(jnp.concatenate(lines), axis), 0, {})
    for k, line in zip(sequence, lines):
        slab = both[:, at : at + len(line)].reshape(len(both), -1)
        found[k] = slab[:, : leaves[k].size].reshape(-1, *leaves[k].shape)
        at += len(line)
    numbers = iter(range(len(leaves)))
    return jax.tree.map(lambda _: found[next(numbers)], shard)


def joined_by_halves(pieces, combine):
    while len(jax.tree.leaves(pieces)[0]) > 1:
        pieces = jax.vmap(combine)(
            *(jax.tree.map(lambda part: part[side::2], pieces) for side in (0, 1))
        )
    return jax.tree.map(lambda part: part[0], pieces)


def prefix(shard, axis, combine, identity):
    peers, mine = (lax.axis_size(axis), lax.axis_index(axis))
    passed = jnp.arange(peers) < mine

    def kept(part, zero, own):
        part = jnp.where(
            passed.reshape(-1, *(1 for _ in own.shape)), part, jnp.asarray(zero, own.dtype)
        )
        return part

    pieces = all_in_one(shard, axis)
    return joined_by_halves(jax.tree.map(kept, pieces, identity, shard), combine)


def of_everyone(shard, axis):
    everything = copy_for_each(shard, axis)
    return jnp.sum(everything, axis=0)


def join_pair(earlier, later):
    return (earlier[0] * later[0], later[0] * earlier[1] + later[1])


def per_device(fade_rate, update_in, norm_gain):
    total_length = fade_rate.shape[1] * lax.axis_size("sp")
    keep = jnp.exp(-fade_rate / total_length)
    push = update_in.astype(jnp.float32) * total_length ** (-0.5)
    steps = -fade_rate / total_length
    logs = jnp.sum(steps, axis=1, keepdims=True) - jnp.cumsum(steps, axis=1)
    summary = (jnp.exp(jnp.sum(steps, axis=1)), jnp.sum(jnp.exp(logs) * push, axis=1))
    entering_forward = prefix(
        summary, "sp", join_pair, (jnp.ones_like(keep[:, 0]), jnp.zeros_like(push[:, 0]))
    )
    started = push.at[:, 0].add(keep[:, 0] * entering_forward[1])
    forward = lax.associative_scan(join_pair, (keep, started), axis=1)[1]
    power = of_everyone(jnp.sum(forward * forward, axis=-1, keepdims=True), "tp") / (
        forward.shape[-1] * lax.axis_size("tp")
    )
    mixed_out = (forward * lax.rsqrt(power + 1e-06) * norm_gain).astype(jnp.bfloat16)
    return mixed_out


def solution(mesh):
    placed = (P(None, "sp", "tp"), P(None, "sp", "tp"), P("tp"))
    return jax.shard_map(
        per_device, mesh=mesh, in_specs=placed, out_specs=P(None, "sp", "tp"), check_vma=False
    )
```

profile of v0, /device:TPU:1, one launch (start us, length us, event | category | flops | bytes accessed | tf_op | source)
XLA Modules:
  0.0 112.5 jit_solution(8689377111815746045)
XLA Ops:
  0.0 2.0 %fusion.19 = (f32[1,1024,512]{2,1,0:T(8,128)S(1)}, f32[512]{0:T(512)S(1)}, f32[1,1024,512]{2,1,0:T(8,128)S(1)}) fusion(f32[1,1024,512]{2,1,0:T(8,128)} %param.5), kind=kLoop, calls=%fused_computation.76 | loop fusion | flops 1572352 | bytes 6293504 | tf_op jit(solution)/shard_map/exp | solution.py:62
  3.3 2.5 %copy.8 = f32[1,512,8,128]{1,3,2,0:T(8,128)} copy(f32[1,512,8,128]{1,2,3,0:T(8,128)S(1)} %fusion.3) | data formatting | bytes 4194304 | tf_op jit(solution)/shard_map/reduce-window
  5.9 3.5 %fusion = (f32[512]{0:T(512)S(1)}, f32[1,1024,512]{2,1,0:T(8,128)}) fusion(f32[1,512,8,128]{1,3,2,0:T(8,128)} %copy.8, f32[512,8]{0,1:T(8,128)S(1)} %slice_bitcast_fusion, f32[512]{0:T(512)S(1)} %get-tuple-element.20, bf16[1,1024,512]{2,1,0:T(8,128)(2,1)S(1)} %copy-done.5), kind=kLoop, calls=%fused_computation.1 | loop fusion | flops 3145216 | bytes 5263360 | tf_op jit(solution)/shard_map/reduce_sum | solution.py:66
  10.2 19.6 %all-to-all-start = ((f32[64,2,512]{2,1,0:T(2,128)}), f32[64,2,512]{2,1,0:T(2,128)S(1)}, u32[]{:S(2)}, u32[]{:S(2)}) async-start(f32[64,2,512]{2,1,0:T(2,128)} %broadcast_in_dim.30), calls=%async_computation | async-start | bytes 524288 | tf_op jit(solution)/shard_map/all_to_all | solution.py:9
  29.8 3.5 %slice.372 = f32[1,512,512]{2,1,0:T(8,128)} slice(f32[1,1024,512]{2,1,0:T(8,128)S(1)} %get-tuple-element.19), slice={[0:1:1], [0:1023:2], [0:512:1]} | slice | bytes 2097152 | tf_op jit(solution)/shard_map/slice | solution.py:71
  33.3 3.5 %slice.368 = f32[1,512,512]{2,1,0:T(8,128)} slice(f32[1,1024,512]{2,1,0:T(8,128)S(1)} %get-tuple-element.19), slice={[0:1:1], [1:1024:2], [0:512:1]} | slice | bytes 2097152 | tf_op jit(solution)/shard_map/slice | solution.py:71
  37.8 6.2 %all-to-all-done = f32[64,2,512]{2,1,0:T(2,128)S(1)} async-done(((f32[64,2,512]{2,1,0:T(2,128)}), f32[64,2,512]{2,1,0:T(2,128)S(1)}, u32[]{:S(2)}, u32[]{:S(2)}) %all-to-all-start) | async-done | bytes 262176 | tf_op jit(solution)/shard_map/all_to_all | solution.py:9
  45.3 1.3 %scatter-add.4 = f32[1,1024,512]{2,1,0:T(8,128)} dynamic-update-slice(f32[1,1024,512]{2,1,0:T(8,128)} %get-tuple-element.25, f32[1,1,512]{2,1,0:T(1,128)S(1)} %fusion.17, s32[]{:T(128)} %constant.49.clone.1, s32[]{:T(128)} %constant.49.clone.1, s32[]{:T(128)} %constant.49.clone.1) | dynamic-update-slice | bytes 4100 | tf_op jit(solution)/shard_map/scatter-add | solution.py:70
  46.7 6.5 %slice.440 = f32[1,511,512]{2,1,0:T(8,128)} slice(f32[1,1024,512]{2,1,0:T(8,128)} %scatter-add.4), slice={[0:1:1], [2:1024:2], [0:512:1]} | slice | bytes 2093056 | tf_op jit(solution)/shard_map/slice | solution.py:71
  53.2 3.5 %slice.370 = f32[1,512,512]{2,1,0:T(8,128)} slice(f32[1,1024,512]{2,1,0:T(8,128)S(1)} %copy-done), slice={[0:1:1], [1:1024:2], [0:512:1]} | slice | bytes 2097152 | tf_op jit(solution)/shard_map/slice | solution.py:71
  56.7 3.5 %slice.369 = f32[1,512,512]{2,1,0:T(8,128)} slice(f32[1,1024,512]{2,1,0:T(8,128)S(1)} %copy-done), slice={[0:1:1], [0:1023:2], [0:512:1]} | slice | bytes 2097152 | tf_op jit(solution)/shard_map/slice | solution.py:71
  60.2 2.7 %fusion.20 = (f32[1,512,512]{2,1,0:T(8,128)S(1)}, f32[1,512,512]{2,1,0:T(8,128)S(1)}) fusion(f32[1,512,512]{2,1,0:T(8,128)} %slice.372, f32[1,512,512]{2,1,0:T(8,128)} %slice.368, f32[1,512,512]{2,1,0:T(8,128)} %slice.370, f32[1,512,512]{2,1,0:T(8,128)} %slice.369), kind=kLoop, calls=%fused_computation.77 | loop fusion | flops 786432 | bytes 6291456 | tf_op jit(solution)/shard_map/mul | solution.py:57
  62.8 2.1 %slice.378 = f32[1,256,512]{2,1,0:T(8,128)} slice(f32[1,512,512]{2,1,0:T(8,128)S(1)} %get-tuple-element.22), slice={[0:1:1], [0:511:2], [0:512:1]} | slice | bytes 1048576 | tf_op jit(solution)/shard_map/slice | solution.py:71
  64.9 2.1 %slice.374 = f32[1,256,512]{2,1,0:T(8,128)} slice(f32[1,512,512]{2,1,0:T(8,128)S(1)} %get-tuple-element.22), slice={[0:1:1], [1:512:2], [0:512:1]} | slice | bytes 1048576 | tf_op jit(solution)/shard_map/slice | solution.py:71
  67.0 2.1 %slice.373 = f32[1,255,512]{2,1,0:T(8,128)} slice(f32[1,512,512]{2,1,0:T(8,128)S(1)} %get-tuple-element.22), slice={[0:1:1], [2:512:2], [0:512:1]} | slice | bytes 1044480 | tf_op jit(solution)/shard_map/slice | solution.py:71
  69.7 2.1 %slice.376 = f32[1,256,512]{2,1,0:T(8,128)} slice(f32[1,512,512]{2,1,0:T(8,128)S(1)} %get-tuple-element.23), slice={[0:1:1], [1:512:2], [0:512:1]} | slice | bytes 1048576 | tf_op jit(solution)/shard_map/slice | solution.py:71
  71.8 2.1 %slice.375 = f32[1,256,512]{2,1,0:T(8,128)} slice(f32[1,512,512]{2,1,0:T(8,128)S(1)} %get-tuple-element.23), slice={[0:1:1], [0:511:2], [0:512:1]} | slice | bytes 1048576 | tf_op jit(solution)/shard_map/slice | solution.py:71
  73.8 1.6 %fusion.21 = (f32[1,256,512]{2,1,0:T(8,128)S(1)}, f32[1,256,512]{2,1,0:T(8,128)S(1)}) fusion(f32[1,256,512]{2,1,0:T(8,128)S(1)} %copy-done.4, f32[1,256,512]{2,1,0:T(8,128)} %slice.374, f32[1,256,512]{2,1,0:T(8,128)} %slice.376, f32[1,256,512]{2,1,0:T(8,128)} %slice.375), kind=kLoop, calls=%fused_computation.78 | loop fusion | flops 393216 | bytes 3145728 | tf_op jit(solution)/shard_map/mul | solution.py:57
  75.7 1.4 %slice.380 = f32[1,128,512]{2,1,0:T(8,128)} slice(f32[1,256,512]{2,1,0:T(8,128)S(1)} %get-tuple-element.26), slice={[0:1:1], [1:256:2], [0:512:1]} | slice | bytes 524288 | tf_op jit(solution)/shard_map/slice | solution.py:71
  83.5 2.1 %pad.80 = f32[1,512,512]{2,1,0:T(8,128)S(1)} pad(f32[1,256,512]{2,1,0:T(8,128)} %add.194, f32[]{:T(128)} %constant.47.clone.1), padding=0_0_0x1_0_1x0_0_0 | pad | bytes 1572868 | tf_op jit(solution)/shard_map/pad | solution.py:71
  87.6 4.8 %pad.81 = f32[1,1024,512]{2,1,0:T(8,128)} pad(f32[1,512,512]{2,1,0:T(8,128)S(1)} %pad_maximum_fusion, f32[]{:T(128)} %constant.47.clone.1), padding=0_0_0x0_1_1x0_0_0 | pad | bytes 3145732 | tf_op jit(solution)/shard_map/pad | solution.py:71
  92.5 4.8 %pad.82 = f32[1,1024,512]{2,1,0:T(8,128)} pad(f32[1,512,512]{2,1,0:T(8,128)S(1)} %copy-done.2, f32[]{:T(128)} %constant.47.clone.1), padding=0_0_0x1_0_1x0_0_0 | pad | bytes 3145732 | tf_op jit(solution)/shard_map/pad | solution.py:71
  97.3 2.5 %multiply_reduce_fusion = (f32[1024]{0:T(1024)S(1)}, f32[1,1024,512]{2,1,0:T(8,128)S(1)}) fusion(f32[1,1024,512]{2,1,0:T(8,128)} %pad.81, f32[1,1024,512]{2,1,0:T(8,128)} %pad.82), kind=kLoop, calls=%fused_computation.8 | loop fusion | flops 1571840 | bytes 6295552 | tf_op jit(solution)/shard_map/reduce_sum | solution.py:72
  99.8 11.4 %all_to_all.10 = f32[8,1,1024,1]{2,3,1,0:T(1,128)S(1)} all-to-all(f32[8,1,1024,1]{2,3,1,0:T(1,128)S(1)} %broadcast_in_dim.33), channel_id=1, replica_groups=mesh['sp'=64,'tp'=8] {'tp'}, dimensions={0} | all-to-all | bytes 65536 | tf_op jit(solution)/shard_map/all_to_all | solution.py:9
  (131 shorter events, 14.5 us)
Async XLA Ops:
  3.3 2.6 %copy-start.5 = (bf16[1,1024,512]{2,1,0:T(8,128)(2,1)S(1)}, bf16[1,1024,512]{2,1,0:T(8,128)(2,1)}, u32[]{:S(2)}) copy-start(bf16[1,1024,512]{2,1,0:T(8,128)(2,1)} %param.6) | copy-start | bytes 3145732
  10.2 33.8 %all-to-all-start = ((f32[64,2,512]{2,1,0:T(2,128)}), f32[64,2,512]{2,1,0:T(2,128)S(1)}, u32[]{:S(2)}, u32[]{:S(2)}) async-start(f32[64,2,512]{2,1,0:T(2,128)} %broadcast_in_dim.30), calls=%async_computation | async-start | bytes 524288 | tf_op jit(solution)/shard_map/all_to_all | solution.py:9
  46.7 6.5 %copy-start = (f32[1,1024,512]{2,1,0:T(8,128)S(1)}, f32[1,1024,512]{2,1,0:T(8,128)}, u32[]{:S(2)}) copy-start(f32[1,1024,512]{2,1,0:T(8,128)} %scatter-add.4) | copy-start | bytes 6291460
  69.1 4.7 %copy-start.4 = (f32[1,256,512]{2,1,0:T(8,128)S(1)}, f32[1,256,512]{2,1,0:T(8,128)}, u32[]{:S(2)}) copy-start(f32[1,256,512]{2,1,0:T(8,128)} %slice.378) | copy-start | bytes 1572868
  82.0 1.1 copy-start.3
  85.6 1.4 %copy-start.1 = (f32[1,511,512]{2,1,0:T(8,128)S(1)}, f32[1,511,512]{2,1,0:T(8,128)}, u32[]{:S(2)}) copy-start(f32[1,511,512]{2,1,0:T(8,128)} %slice.440) | copy-start | bytes 3139588
  87.6 4.8 %copy-start.2 = (f32[1,512,512]{2,1,0:T(8,128)S(1)}, f32[1,512,512]{2,1,0:T(8,128)}, u32[]{:S(2)}) copy-start(f32[1,512,512]{2,1,0:T(8,128)} %add.196) | copy-start | bytes 3145732
  97.3 14.0 %copy-start.6 = (f32[512]{0:T(512)S(1)}, f32[512]{0:T(512)}, u32[]{:S(2)}) copy-start(f32[512]{0:T(512)} %param.7) | copy-start | bytes 6148
where the time goes:
time: 113 us
  local copies, waits for them, and re-layouts  54 us (48%)
  other arithmetic  20.6 us (18%)
  starting transfers between devices  19.6 us (17%)
  blocking collectives  11.4 us (10%)
  waiting for transfers between devices  6.22 us (6%)
    slice x59, local copies, waits for them, and re-layouts, per_device(): forward = lax.associative_scan(join_pair, (keep, started), axis=1)[1]  36.9 us
    all_to_all x1, starting transfers between devices, copy_for_each(): return lax.all_to_all(copies, axis, split_axis=0, concat_axis=0, tiled=True)  19.6 us
    pad x18, local copies, waits for them, and re-layouts, per_device(): forward = lax.associative_scan(join_pair, (keep, started), axis=1)[1]  12.2 us
    all_to_all x1, blocking collectives, copy_for_each(): return lax.all_to_all(copies, axis, split_axis=0, concat_axis=0, tiled=True)  11.4 us
    all_to_all x1, waiting for transfers between devices, copy_for_each(): return lax.all_to_all(copies, axis, split_axis=0, concat_axis=0, tiled=True)  6.22 us
    mul x12, other arithmetic, join_pair(): return (earlier[0] * later[0], later[0] * earlier[1] + later[1])  5.62 us
    reduce_sum x1, other arithmetic, per_device(): jnp.sum(jnp.exp(logs) * push, axis=1)  3.47 us
    another operation x3, local copies, waits for them, and re-layouts  2.55 us
  transfers between devices with their start and end apart: 1, of which 1 were waited for; matrix products, arithmetic and copies ran while one was open for 7% of the time, Pallas kernels for 0%

commit v1 on v0

v1 whole, which is shorter than its diff:
```python
import functools
import math

import jax
import jax.numpy as jnp
from jax import lax
from jax.experimental import pallas as pl
from jax.experimental.pallas import tpu as pltpu
from jax.sharding import PartitionSpec as P

LANES = 128
F32, BF16 = jnp.float32, jnp.bfloat16
VMEM = pl.BlockSpec(memory_space=pltpu.VMEM)
HBM = pl.BlockSpec(memory_space=pltpu.HBM)
LOG2E = math.log2(math.e)


def pieces(x):
    high = x.astype(BF16)
    return high, (x - high.astype(F32)).astype(BF16)


def local_kernel(block, peers, rate, fade, update, decay, inner, message, fades, updates, sems):
    length, width = fade.shape
    blocks = length // block
    copies = []
    for b in range(blocks):
        rows = pl.ds(b * block, block)
        pair = (
            pltpu.make_async_copy(fade.at[rows], fades.at[rows], sems.at[0, b]),
            pltpu.make_async_copy(update.at[rows], updates.at[rows], sems.at[1, b]),
        )
        for copy in pair:
            copy.start()
        copies.append(pair)
    row = lax.broadcasted_iota(jnp.int32, (block, block), 0)
    column = lax.broadcasted_iota(jnp.int32, (block, block), 1)
    upto = jnp.where(column <= row, 1.0, 0.0).astype(BF16)

    def running(*terms):
        return sum(jnp.dot(upto, t, preferred_element_type=F32) for t in terms)

    faded = jnp.zeros((1, width), F32)
    pushed = jnp.zeros((1, width), F32)
    for b in range(blocks):
        rows = pl.ds(b * block, block)
        copies[b][0].wait()
        f = fades[rows, :]
        total = (running(*pieces(f)) + faded) * rate
        faded = faded + jnp.sum(f, axis=0, keepdims=True)
        decay[rows, :] = jnp.exp2(-total)
        growth = jnp.exp2(total) - 1.0
        copies[b][1].wait()
        u = updates[rows, :]
        so_far = running(u, *pieces(u.astype(F32) * growth)) + pushed
        inner[rows, :] = so_far
        pushed = so_far[block - 1 : block, :]
    cut = [slice(g * LANES, (g + 1) * LANES) for g in range(width // LANES)]
    tile = jnp.concatenate([faded[:, c] for c in cut] + [pushed[:, c] for c in cut], axis=0)
    for p in range(peers):
        message[p] = tile


def carry_kernel(rate, copies, tile, decay, inner, gathered, forward, message):
    length, width = decay.shape
    peers, high, lanes = gathered.shape
    groups = width // lanes
    me = lax.axis_index("sp")
    states, keeps = [], []
    for first in range(0, peers, 8):
        state = keep = None
        for p in range(first, first + 8):
            t = gathered[p]
            k = pltpu.roll(jnp.exp2(t * -rate), groups, 0)
            k = jnp.where(p < me, k, 1.0)
            t = jnp.where(p < me, t, 0.0)
            state = t * k if state is None else (state + t) * k
            keep = k if keep is None else keep * k
        states.append(state)
        keeps.append(keep)
    state = states[0]
    for s, k in zip(states[1:], keeps[1:]):
        state = state * k + s
    entering = [state[groups + g : groups + g + 1, :] for g in range(groups)]
    ones = jnp.ones((8, lanes), BF16)
    row = lax.broadcasted_iota(jnp.int32, (8, lanes), 0)
    out = jnp.zeros((8, lanes), F32)
    for s in range(length // lanes):
        rows = pl.ds(s * lanes, lanes)
        power = None
        for g in range(groups):
            at = pl.ds(g * lanes, lanes)
            f = decay[rows, at] * (inner[rows, at] + entering[g])
            forward[rows, at] = f
            power = f * f if power is None else power + f * f
        sums = sum(
            lax.dot_general(ones, t, (((1,), (1,)), ((), ())), preferred_element_type=F32)
            for t in pieces(power)
        )
        out = jnp.where(row == s, sums, out)
    for p in range(copies):
        message[p] = out


def norm_kernel(channels, total_length, forward, powers, gain, out, staged, sems):
    length, width = forward.shape
    lanes = powers.shape[-1]
    power = powers[0]
    for p in range(1, powers.shape[0]):
        power = power + powers[p]
    scale = lax.rsqrt(power * (1.0 / (channels * total_length)) + 1e-06) * total_length ** (-0.5)
    scale = scale.T
    copies = []
    for s in range(length // lanes):
        rows = pl.ds(s * lanes, lanes)
        staged[rows, :] = (forward[rows, :] * scale[:, s : s + 1] * gain[...]).astype(BF16)
        copies.append(pltpu.make_async_copy(staged.at[rows], out.at[rows], sems.at[s]))
        copies[-1].start()
    for copy in copies:
        copy.wait()


def per_device(fade_rate, update_in, norm_gain):
    _, length, width = fade_rate.shape
    stretches, parts = lax.axis_size("sp"), lax.axis_size("tp")
    total_length = length * stretches
    rate = LOG2E / total_length
    block = 256
    blocks = length // block
    limit = pltpu.CompilerParams(vmem_limit_bytes=24 * 1024 * 1024)
    wide = jax.ShapeDtypeStruct((length, width), F32)
    decay, inner, summary = pl.pallas_call(
        functools.partial(local_kernel, block, stretches, rate),
        out_shape=(wide, wide, jax.ShapeDtypeStruct((stretches, 8, LANES), F32)),
        in_specs=[HBM, HBM],
        out_specs=(VMEM, VMEM, VMEM),
        scratch_shapes=[
            pltpu.VMEM((length, width), F32),
            pltpu.VMEM((length, width), BF16),
            pltpu.SemaphoreType.DMA((2, blocks)),
        ],
        compiler_params=limit,
        name="local",
    )(*(pltpu.with_memory_space_constraint(a[0], pltpu.HBM) for a in (fade_rate, update_in)))
    gathered = lax.all_to_all(summary, "sp", 0, 0, tiled=True)
    forward, power = pl.pallas_call(
        functools.partial(carry_kernel, rate, parts, 8),
        out_shape=(wide, jax.ShapeDtypeStruct((parts, 8, LANES), F32)),
        in_specs=[VMEM, VMEM, VMEM],
        out_specs=(VMEM, VMEM),
        compiler_params=limit,
        name="carry",
    )(decay, inner, gathered)
    powers = lax.all_to_all(power, "tp", 0, 0, tiled=True)
    out = pl.pallas_call(
        functools.partial(norm_kernel, width * parts, total_length),
        out_shape=jax.ShapeDtypeStruct((length, width), BF16),
        in_specs=[VMEM, VMEM, VMEM],
        out_specs=HBM,
        scratch_shapes=[
            pltpu.VMEM((length, width), BF16),
            pltpu.SemaphoreType.DMA((length // LANES,)),
        ],
        compiler_params=limit,
        name="norm",
    )(forward, powers, norm_gain[None])
    return out[None]


def solution(mesh):
    placed = (P(None, "sp", "tp"), P(None, "sp", "tp"), P("tp"))
    return jax.shard_map(
        per_device, mesh=mesh, in_specs=placed, out_specs=P(None, "sp", "tp"), check_vma=False
    )
```

time: 113 us -> 51.5 us (0.46)
  local copies, waits for them, and re-layouts: 54 us -> 0.01 us
  blocking collectives: 11.4 us -> 45 us
  other arithmetic: 20.6 us -> 0 us
  starting transfers between devices: 19.6 us -> 0 us
  Pallas kernels: 0 us -> 6.33 us
  waiting for transfers between devices: 6.22 us -> 0 us
    slice x59 -> x0, local copies, waits for them, and re-layouts: 36.9 us -> none  [per_device(): forward = lax.associative_scan(join_pair, (keep, started), axis=1)[1]]
    all_to_all x1 -> x2, blocking collectives: 11.4 us -> 45 us  [the longest x1 33.6 us: per_device(): gathered = lax.all_to_all(summary, 'sp', 0, 0, tiled=True)]
    all_to_all x1 -> x0, starting transfers between devices: 19.6 us -> none  [copy_for_each(): return lax.all_to_all(copies, axis, split_axis=0, concat_axis=0, tiled=True)]
    pad x18 -> x0, local copies, waits for them, and re-layouts: 12.2 us -> none  [per_device(): forward = lax.associative_scan(join_pair, (keep, started), axis=1)[1]]
    pallas_call x0 -> x3, Pallas kernels: none -> 6.33 us  [the longest x1 4.48 us: per_device(): pl.pallas_call(functools.partial(local_kernel, block, stretches, rate), o...]
    all_to_all x1 -> x0, waiting for transfers between devices: 6.22 us -> none  [copy_for_each(): return lax.all_to_all(copies, axis, split_axis=0, concat_axis=0, tiled=True)]
    reduce_sum x3 -> x0, other arithmetic: 6.03 us -> none  [the longest x1 3.47 us: per_device(): jnp.sum(jnp.exp(logs) * push, axis=1)]
    mul x12 -> x0, other arithmetic: 5.62 us -> none  [join_pair(): return (earlier[0] * later[0], later[0] * earlier[1] + later[1])]
  transfers between devices with their start and end apart: 1 -> 0, of which waited for: 1 -> 0; matrix products, arithmetic and copies ran while one was open for 7% -> 0% of each run, Pallas kernels for 0% -> 0%
where the time goes in v1:
time: 51.5 us; the launch traced here: 51.4 us
  blocking collectives  45 us (87%)
  Pallas kernels  6.33 us (12%)
    all_to_all x1, blocking collectives, per_device(): gathered = lax.all_to_all(summary, 'sp', 0, 0, tiled=True)  33.6 us
    all_to_all x1, blocking collectives, per_device(): powers = lax.all_to_all(power, 'tp', 0, 0, tiled=True)  11.4 us
    pallas_call x1, Pallas kernels, per_device(): pl.pallas_call(functools.partial(local_kernel, block, stretches, rate), o...  4.48 us
    pallas_call x1, Pallas kernels, per_device(): pl.pallas_call(functools.partial(norm_kernel, width * parts, total_length...  1.29 us

profile of v1, /device:TPU:1, one launch (start us, length us, event | category | flops | bytes accessed | tf_op | source)
XLA Modules:
  0.0 51.4 jit_solution(15034118779596365577)
XLA Ops:
  0.0 4.5 %local.1 = (f32[1024,512]{1,0:T(8,128)S(1)}, f32[1024,512]{1,0:T(8,128)S(1)}, f32[64,8,128]{2,1,0:T(8,128)S(1)}) custom-call(f32[1024,512]{1,0:T(8,128)} %bitcast.5, bf16[1024,512]{1,0:T(8,128)(2,1)} %bitcast.6), custom_call_target="tpu_custom_call" | custom-call | tf_op jit(solution)/shard_map/local/pallas_call | solution.py:132
  4.5 33.6 %all_to_all.10.gathered = f32[64,8,128]{2,1,0:T(8,128)S(1)} all-to-all(f32[64,8,128]{2,1,0:T(8,128)S(1)} %get-tuple-element.12), channel_id=1, replica_groups=mesh['sp'=64,'tp'=8] {'sp'}, dimensions={0} | all-to-all | bytes 524288 | tf_op jit(solution)/shard_map/all_to_all | solution.py:145
  38.1 0.0 copy-start
  38.1 0.6 %carry.1 = (f32[1024,512]{1,0:T(8,128)S(1)}, f32[8,8,128]{2,1,0:T(8,128)S(1)}) custom-call(f32[1024,512]{1,0:T(8,128)S(1)} %get-tuple-element.10.decay, f32[1024,512]{1,0:T(8,128)S(1)} %get-tuple-element.11.inner, f32[64,8,128]{2,1,0:T(8,128)S(1)} %all_to_all.10.gathered), custom_call_target="tpu_custom_call" | custom-call | tf_op jit(solution)/shard_map/carry/pallas_call | solution.py:146
  38.7 11.4 %all_to_all.11.powers = f32[8,8,128]{2,1,0:T(8,128)S(1)} all-to-all(f32[8,8,128]{2,1,0:T(8,128)S(1)} %get-tuple-element.14), channel_id=1, replica_groups=mesh['sp'=64,'tp'=8] {'tp'}, dimensions={0} | all-to-all | bytes 65536 | tf_op jit(solution)/shard_map/all_to_all | solution.py:154
  50.1 0.0 copy-done
  50.1 1.3 %norm.1 = bf16[1024,512]{1,0:T(8,128)(2,1)} custom-call(f32[1024,512]{1,0:T(8,128)S(1)} %get-tuple-element.13.forward, f32[8,8,128]{2,1,0:T(8,128)S(1)} %all_to_all.11.powers, f32[1,512]{1,0:T(1,128)S(1)} %bitcast.4), custom_call_target="tpu_custom_call" | custom-call | tf_op jit(solution)/shard_map/norm/pallas_call | solution.py:155
Async XLA Ops:
  38.1 12.0 %copy-start = (f32[512]{0:T(512)S(1)}, f32[512]{0:T(512)}, u32[]{:S(2)}) copy-start(f32[512]{0:T(512)} %param.5) | copy-start | bytes 6148

commit v2 on v1

v2 whole, which is shorter than its diff:
```python
import functools
import math

import jax
import jax.numpy as jnp
from jax import lax
from jax.experimental import pallas as pl
from jax.experimental.pallas import tpu as pltpu
from jax.sharding import PartitionSpec as P

LANES = 128
F32, BF16 = jnp.float32, jnp.bfloat16
VMEM = pl.BlockSpec(memory_space=pltpu.VMEM)
HBM = pl.BlockSpec(memory_space=pltpu.HBM)
LOG2E = math.log2(math.e)


def pieces(x):
    high = x.astype(BF16)
    return high, (x - high.astype(F32)).astype(BF16)


def as_tile(*rows):
    lines = [r[:, at : at + LANES] for r in rows for at in range(0, r.shape[1], LANES)]
    return jnp.concatenate(lines, axis=0)


def local_kernel(block, stage, rate, fade, update, decay, inner, marks, message, fades, updates, sems):
    length, width = fade.shape
    half = 2 * LANES
    copies = []
    for b in range(length // stage):
        rows = pl.ds(b * stage, stage)
        pair = (
            pltpu.make_async_copy(fade.at[rows], fades.at[rows], sems.at[0, b]),
            pltpu.make_async_copy(update.at[rows], updates.at[rows], sems.at[1, b]),
        )
        for copy in pair:
            copy.start()
        copies.append(pair)
    row = lax.broadcasted_iota(jnp.int32, (block, block), 0)
    column = lax.broadcasted_iota(jnp.int32, (block, block), 1)
    upto = jnp.where(column <= row, 1.0, 0.0).astype(BF16)
    twice = jnp.concatenate([upto, upto], axis=1)

    kept, ended = None, None
    for b in range(length // block):
        rows = pl.ds(b * block, block)
        if b * block % stage == 0:
            for copy in copies[b * block // stage]:
                copy.wait()
        keeps, ends = [], []
        for h in range(width // half):
            at = pl.ds(h * half, half)
            f = fades[rows, at]
            total = jnp.dot(upto, f.astype(BF16), preferred_element_type=F32) * rate
            decay[rows, at] = jnp.exp2(-total)
            u = updates[rows, at]
            more = (u.astype(F32) * (jnp.exp2(total) - 1.0)).astype(BF16)
            so_far = jnp.dot(twice, jnp.concatenate([u, more], axis=0), preferred_element_type=F32)
            inner[rows, at] = so_far
            keep = jnp.exp2(jnp.sum(f, axis=0, keepdims=True) * -rate)
            keeps.append(keep)
            ends.append(so_far[block - 1 :, :] * keep)
        keep, end = (jnp.concatenate(r, axis=1) for r in (keeps, ends))
        marks[b] = as_tile(keep, end)
        kept, ended = (keep, end) if kept is None else (kept * keep, ended * keep + end)
    tile = as_tile(kept, ended)
    for p in range(message.shape[0]):
        message[p] = tile


def carry_kernel(decay, inner, marks, gathered, forward, message):
    length, width = decay.shape
    peers, high, lanes = gathered.shape
    groups = width // lanes
    blocks = marks.shape[0]
    block = length // blocks
    row = lax.broadcasted_iota(jnp.int32, (high, lanes), 0)
    earlier = jnp.where(row >= groups, lax.axis_index("sp"), 0)
    states, keeps = [], []
    for first in range(0, peers, 8):
        state = keep = None
        for p in range(first, first + 8):
            t = gathered[p]
            k = jnp.where(p < earlier, pltpu.roll(t, groups, 0), 1.0)
            t = jnp.where(p < earlier, t, 0.0)
            state = t if state is None else state * k + t
            keep = k if keep is None else keep * k
        states.append(state)
        keeps.append(keep)
    state = states[0]
    for s, k in zip(states[1:], keeps[1:]):
        state = state * k + s
    ones = jnp.ones((8, lanes), BF16)
    out = jnp.zeros((8, lanes), F32)
    for b in range(blocks):
        rows = pl.ds(b * block, block)
        power = None
        for g in range(groups):
            at = pl.ds(g * lanes, lanes)
            f = decay[rows, at] * (inner[rows, at] + state[groups + g : groups + g + 1, :])
            forward[rows, at] = f
            power = f * f if power is None else power + f * f
        sums = sum(
            lax.dot_general(ones, t, (((1,), (1,)), ((), ())), preferred_element_type=F32)
            for t in pieces(power)
        )
        out = jnp.where(row == b, sums, out)
        state = state * pltpu.roll(marks[b], groups, 0) + marks[b]
    for p in range(message.shape[0]):
        message[p] = out


def norm_kernel(channels, total_length, forward, powers, gain, out, staged, sems):
    length, width = forward.shape
    lanes = powers.shape[-1]
    power = powers[0]
    for p in range(1, powers.shape[0]):
        power = power + powers[p]
    scale = lax.rsqrt(power * (1.0 / (channels * total_length)) + 1e-06) * total_length ** (-0.5)
    scale = scale.T
    copies = []
    for s in range(length // lanes):
        rows = pl.ds(s * lanes, lanes)
        staged[rows, :] = (forward[rows, :] * scale[:, s : s + 1] * gain[...]).astype(BF16)
        copies.append(pltpu.make_async_copy(staged.at[rows], out.at[rows], sems.at[s]))
        copies[-1].start()
    for copy in copies:
        copy.wait()


def per_device(fade_rate, update_in, norm_gain):
    _, length, width = fade_rate.shape
    stretches, parts = lax.axis_size("sp"), lax.axis_size("tp")
    total_length = length * stretches
    rate = LOG2E / total_length
    block, stage = LANES, 512
    blocks = length // block
    limit = pltpu.CompilerParams(vmem_limit_bytes=24 * 1024 * 1024)
    wide = jax.ShapeDtypeStruct((length, width), F32)

    def tiles(count):
        return jax.ShapeDtypeStruct((count, 8, LANES), F32)

    decay, inner, marks, summary = pl.pallas_call(
        functools.partial(local_kernel, block, stage, rate),
        out_shape=(wide, wide, tiles(blocks), tiles(stretches)),
        in_specs=[HBM, HBM],
        out_specs=(VMEM, VMEM, VMEM, VMEM),
        scratch_shapes=[
            pltpu.VMEM((length, width), F32),
            pltpu.VMEM((length, width), BF16),
            pltpu.SemaphoreType.DMA((2, length // stage)),
        ],
        compiler_params=limit,
        name="local",
    )(*(pltpu.with_memory_space_constraint(a[0], pltpu.HBM) for a in (fade_rate, update_in)))
    gathered = lax.all_to_all(summary, "sp", 0, 0, tiled=True)
    forward, power = pl.pallas_call(
        carry_kernel,
        out_shape=(wide, tiles(parts)),
        in_specs=[VMEM, VMEM, VMEM, VMEM],
        out_specs=(VMEM, VMEM),
        compiler_params=limit,
        name="carry",
    )(decay, inner, marks, gathered)
    powers = lax.all_to_all(power, "tp", 0, 0, tiled=True)
    out = pl.pallas_call(
        functools.partial(norm_kernel, width * parts, total_length),
        out_shape=jax.ShapeDtypeStruct((length, width), BF16),
        in_specs=[VMEM, VMEM, VMEM],
        out_specs=HBM,
        scratch_shapes=[
            pltpu.VMEM((length, width), BF16),
            pltpu.SemaphoreType.DMA((length // LANES,)),
        ],
        compiler_params=limit,
        name="norm",
    )(forward, powers, norm_gain[None])
    return out[None]


def solution(mesh):
    placed = (P(None, "sp", "tp"), P(None, "sp", "tp"), P("tp"))
    return jax.shard_map(
        per_device, mesh=mesh, in_specs=placed, out_specs=P(None, "sp", "tp"), check_vma=False
    )
```

time: 51.5 us -> 49.6 us (0.963)
  Pallas kernels: 6.33 us -> 4.42 us
    pallas_call x2, Pallas kernels: 5.04 us -> 3.13 us  [the longest x1 2.59 us: per_device(): pl.pallas_call(functools.partial(local_kernel, block, stage, rate), out_s...]
where the time goes in v2:
time: 49.6 us; the launch traced here: 49.5 us
  blocking collectives  45 us (91%)
  Pallas kernels  4.42 us (9%)
    all_to_all x1, blocking collectives, per_device(): gathered = lax.all_to_all(summary, 'sp', 0, 0, tiled=True)  33.6 us
    all_to_all x1, blocking collectives, per_device(): powers = lax.all_to_all(power, 'tp', 0, 0, tiled=True)  11.4 us
    pallas_call x1, Pallas kernels, per_device(): pl.pallas_call(functools.partial(local_kernel, block, stage, rate), out_s...  2.59 us
    pallas_call x1, Pallas kernels, per_device(): pl.pallas_call(functools.partial(norm_kernel, width * parts, total_length...  1.29 us

profile of v2, /device:TPU:1, one launch (start us, length us, event | category | flops | bytes accessed | tf_op | source)
XLA Modules:
  0.0 49.5 jit_solution(17189106732835895295)
XLA Ops:
  0.0 2.6 %local.1 = (f32[1024,512]{1,0:T(8,128)S(1)}, f32[1024,512]{1,0:T(8,128)S(1)}, f32[8,8,128]{2,1,0:T(8,128)S(1)}, f32[64,8,128]{2,1,0:T(8,128)S(1)}) custom-call(f32[1024,512]{1,0:T(8,128)} %bitcast.5, bf16[1024,512]{1,0:T(8,128)(2,1)} %bitcast.6), custom_call_target="tpu_custom_call" | custom-call | tf_op jit(solution)/shard_map/local/pallas_call | solution.py:146
  2.6 33.6 %all_to_all.10.gathered = f32[64,8,128]{2,1,0:T(8,128)S(1)} all-to-all(f32[64,8,128]{2,1,0:T(8,128)S(1)} %get-tuple-element.14), channel_id=1, replica_groups=mesh['sp'=64,'tp'=8] {'sp'}, dimensions={0} | all-to-all | bytes 524288 | tf_op jit(solution)/shard_map/all_to_all | solution.py:159
  36.2 0.0 copy-start
  36.2 0.5 %carry.1 = (f32[1024,512]{1,0:T(8,128)S(1)}, f32[8,8,128]{2,1,0:T(8,128)S(1)}) custom-call(f32[1024,512]{1,0:T(8,128)S(1)} %get-tuple-element.11.decay, f32[1024,512]{1,0:T(8,128)S(1)} %get-tuple-element.12.inner, f32[8,8,128]{2,1,0:T(8,128)S(1)} %get-tuple-element.13.marks, f32[64,8,128]{2,1,0:T(8,128)S(1)} %all_to_all.10.gathered), custom_call_target="tpu_custom_call" | custom-call | tf_op jit(solution)/shard_map/carry/pallas_call | solution.py:160
  36.8 11.4 %all_to_all.11.powers = f32[8,8,128]{2,1,0:T(8,128)S(1)} all-to-all(f32[8,8,128]{2,1,0:T(8,128)S(1)} %get-tuple-element.16), channel_id=1, replica_groups=mesh['sp'=64,'tp'=8] {'tp'}, dimensions={0} | all-to-all | bytes 65536 | tf_op jit(solution)/shard_map/all_to_all | solution.py:168
  48.2 0.0 copy-done
  48.2 1.3 %norm.1 = bf16[1024,512]{1,0:T(8,128)(2,1)} custom-call(f32[1024,512]{1,0:T(8,128)S(1)} %get-tuple-element.15.forward, f32[8,8,128]{2,1,0:T(8,128)S(1)} %all_to_all.11.powers, f32[1,512]{1,0:T(1,128)S(1)} %bitcast.4), custom_call_target="tpu_custom_call" | custom-call | tf_op jit(solution)/shard_map/norm/pallas_call | solution.py:169
Async XLA Ops:
  36.2 12.0 %copy-start = (f32[512]{0:T(512)S(1)}, f32[512]{0:T(512)}, u32[]{:S(2)}) copy-start(f32[512]{0:T(512)} %param.5) | copy-start | bytes 6148

commit v3 on v2

--- a/solution.py
+++ b/solution.py
@@ -25,7 +25,7 @@
     return jnp.concatenate(lines, axis=0)
 
 
-def local_kernel(block, stage, rate, fade, update, decay, inner, marks, message, fades, updates, sems):
+def local_kernel(block, stage, rate, fade, update, drop, inner, marks, message, fades, updates, sems):
     length, width = fade.shape
     half = 2 * LANES
     copies = []
@@ -54,7 +54,7 @@
             at = pl.ds(h * half, half)
             f = fades[rows, at]
             total = jnp.dot(upto, f.astype(BF16), preferred_element_type=F32) * rate
-            decay[rows, at] = jnp.exp2(-total)
+            drop[rows, at] = (jnp.exp2(-total) - 1.0).astype(BF16)
             u = updates[rows, at]
             more = (u.astype(F32) * (jnp.exp2(total) - 1.0)).astype(BF16)
             so_far = jnp.dot(twice, jnp.concatenate([u, more], axis=0), preferred_element_type=F32)
@@ -65,33 +65,43 @@
         keep, end = (jnp.concatenate(r, axis=1) for r in (keeps, ends))
         marks[b] = as_tile(keep, end)
         kept, ended = (keep, end) if kept is None else (kept * keep, ended * keep + end)
-    tile = as_tile(kept, ended)
-    for p in range(message.shape[0]):
-        message[p] = tile
-
-
-def carry_kernel(decay, inner, marks, gathered, forward, message):
-    length, width = decay.shape
+    message[...] = as_tile(kept, ended)
+
+
+def prefix_kernel(axis, gathered, keep, end, total):
     peers, high, lanes = gathered.shape
+    row = lax.broadcasted_iota(jnp.int32, (high, lanes), 0)
+    before = jnp.where(row >= high // 2, lax.rem(lax.axis_index(axis), peers), 0)
+    counted = jnp.where(row >= high // 2, peers, 0)
+    own, whole = [], []
+    for first in range(0, peers, 8):
+        for count, links in ((before, own), (counted, whole)):
+            kept = ended = None
+            for p in range(first, min(first + 8, peers)):
+                t = gathered[p]
+                k = jnp.where(p < count, pltpu.roll(t, high // 2, 0), 1.0)
+                t = jnp.where(p < count, t, 0.0)
+                ended = t if ended is None else ended * k + t
+                kept = k if kept is None else kept * k
+            links.append((kept, ended))
+    kept, ended = own[0]
+    for k, e in own[1:]:
+        kept, ended = kept * k, ended * k + e
+    keep[...] = kept
+    end[...] = ended
+    ended = whole[0][1]
+    for k, e in whole[1:]:
+        ended = ended * k + e
+    total[...] = ended
+
+
+def carry_kernel(drop, inner, marks, keep, end, start, forward, message):
+    length, width = drop.shape
+    blocks, _, lanes = marks.shape
     groups = width // lanes
-    blocks = marks.shape[0]
     block = length // blocks
-    row = lax.broadcasted_iota(jnp.int32, (high, lanes), 0)
-    earlier = jnp.where(row >= groups, lax.axis_index("sp"), 0)
-    states, keeps = [], []
-    for first in range(0, peers, 8):
-        state = keep = None
-        for p in range(first, first + 8):
-            t = gathered[p]
-            k = jnp.where(p < earlier, pltpu.roll(t, groups, 0), 1.0)
-            t = jnp.where(p < earlier, t, 0.0)
-            state = t if state is None else state * k + t
-            keep = k if keep is None else keep * k
-        states.append(state)
-        keeps.append(keep)
-    state = states[0]
-    for s, k in zip(states[1:], keeps[1:]):
-        state = state * k + s
+    row = lax.broadcasted_iota(jnp.int32, (8, lanes), 0)
+    state = start[...] * keep[...] + end[...]
     ones = jnp.ones((8, lanes), BF16)
     out = jnp.zeros((8, lanes), F32)
     for b in range(blocks):
@@ -99,7 +109,8 @@
         power = None
         for g in range(groups):
             at = pl.ds(g * lanes, lanes)
-            f = decay[rows, at] * (inner[rows, at] + state[groups + g : groups + g + 1, :])
+            f = inner[rows, at] + state[groups + g : groups + g + 1, :]
+            f = f + f * drop[rows, at].astype(F32)
             forward[rows, at] = f
             power = f * f if power is None else power + f * f
         sums = sum(
@@ -136,6 +147,7 @@
     total_length = length * stretches
     rate = LOG2E / total_length
     block, stage = LANES, 512
+    half = stretches // 2
     blocks = length // block
     limit = pltpu.CompilerParams(vmem_limit_bytes=24 * 1024 * 1024)
     wide = jax.ShapeDtypeStruct((length, width), F32)
@@ -143,11 +155,12 @@
     def tiles(count):
         return jax.ShapeDtypeStruct((count, 8, LANES), F32)
 
-    decay, inner, marks, summary = pl.pallas_call(
+    tile = jax.ShapeDtypeStruct((8, LANES), F32)
+    drop, inner, marks, summary = pl.pallas_call(
         functools.partial(local_kernel, block, stage, rate),
-        out_shape=(wide, wide, tiles(blocks), tiles(stretches)),
+        out_shape=(jax.ShapeDtypeStruct((length, width), BF16), wide, tiles(blocks), tile),
         in_specs=[HBM, HBM],
-        out_specs=(VMEM, VMEM, VMEM, VMEM),
+        out_specs=(VMEM,) * 4,
         scratch_shapes=[
             pltpu.VMEM((length, width), F32),
             pltpu.VMEM((length, width), BF16),
@@ -156,15 +169,37 @@
         compiler_params=limit,
         name="local",
     )(*(pltpu.with_memory_space_constraint(a[0], pltpu.HBM) for a in (fade_rate, update_in)))
-    gathered = lax.all_to_all(summary, "sp", 0, 0, tiled=True)
+    prefix = pl.pallas_call(
+        functools.partial(prefix_kernel, "sp"),
+        out_shape=(tile,) * 3,
+        in_specs=[VMEM],
+        out_specs=(VMEM,) * 3,
+        compiler_params=limit,
+        name="prefix",
+    )
+    early = lax.axis_index("sp") < half
+    halves = [list(range(half)), list(range(half, stretches))]
+
+    def within_half(summary):
+        copies = jnp.broadcast_to(summary, (half, *summary.shape))
+        gathered = lax.all_to_all(copies, "sp", 0, 0, axis_index_groups=halves, tiled=True)
+        return prefix(gathered)
+
+    keep, end, total = lax.cond(
+        early, within_half, lambda s: (jnp.zeros_like(s),) * 3, summary
+    )
+    start = lax.ppermute(total, "sp", [(i, stretches - 1 - i) for i in range(half)])
+    keep, end = lax.cond(
+        early, lambda s, *found: found, lambda s, *_: within_half(s)[:2], summary, keep, end
+    )
     forward, power = pl.pallas_call(
         carry_kernel,
         out_shape=(wide, tiles(parts)),
-        in_specs=[VMEM, VMEM, VMEM, VMEM],
+        in_specs=[VMEM] * 6,
         out_specs=(VMEM, VMEM),
         compiler_params=limit,
         name="carry",
-    )(decay, inner, marks, gathered)
+    )(drop, inner, marks, keep, end, start)
     powers = lax.all_to_all(power, "tp", 0, 0, tiled=True)
     out = pl.pallas_call(
         functools.partial(norm_kernel, width * parts, total_length),

time: 49.6 us -> 44.6 us (0.90)
  blocking collectives: 45 us -> 37.6 us
  starting transfers between devices: 0 us -> 1.29 us
  waiting for transfers between devices: 0 us -> 0.72 us
    all_to_all x1, blocking collectives: 33.6 us -> 27.6 us  [within_half(): lax.all_to_all(copies, 'sp', 0, 0, axis_index_groups=halves, tiled=True)]
    all_to_all x1, blocking collectives: 11.4 us -> 10 us  [per_device(): powers = lax.all_to_all(power, 'tp', 0, 0, tiled=True)]
    ppermute x0 -> x1, starting transfers between devices: none -> 1.29 us  [per_device(): lax.ppermute(total, 'sp', [(i, stretches - 1 - i) for i in range(half)])]
    ppermute x0 -> x1, waiting for transfers between devices: none -> 0.72 us  [per_device(): lax.ppermute(total, 'sp', [(i, stretches - 1 - i) for i in range(half)])]
  transfers between devices with their start and end apart: 0 -> 1, of which waited for: 0 -> 1; matrix products, arithmetic and copies ran while one was open for 0% -> 0% of each run, Pallas kernels for 0% -> 0%
where the time goes in v3:
time: 44.6 us; the launch traced here: 44.4 us
  blocking collectives  37.6 us (84%)
  Pallas kernels  4.64 us (10%)
  starting transfers between devices  1.29 us (3%)
  waiting for transfers between devices  0.72 us (2%)
    all_to_all x1, blocking collectives, within_half(): lax.all_to_all(copies, 'sp', 0, 0, axis_index_groups=halves, tiled=True)  27.6 us
    all_to_all x1, blocking collectives, per_device(): powers = lax.all_to_all(power, 'tp', 0, 0, tiled=True)  10 us
    pallas_call x1, Pallas kernels, per_device(): pl.pallas_call(functools.partial(local_kernel, block, stage, rate), out_s...  2.69 us
    pallas_call x1, Pallas kernels, per_device(): pl.pallas_call(functools.partial(norm_kernel, width * parts, total_length...  1.29 us
    ppermute x1, starting transfers between devices, per_device(): lax.ppermute(total, 'sp', [(i, stretches - 1 - i) for i in range(half)])  1.29 us
  transfers between devices with their start and end apart: 1, of which 1 were waited for; matrix products, arithmetic and copies ran while one was open for 0% of the time, Pallas kernels for 0%

profile of v3, /device:TPU:1, one launch (start us, length us, event | category | flops | bytes accessed | tf_op | source)
XLA Modules:
  0.0 44.4 jit_solution(4243131665861447724)
XLA Ops:
  0.0 2.7 %local.1 = (bf16[1024,512]{1,0:T(8,128)(2,1)S(1)}, f32[1024,512]{1,0:T(8,128)S(1)}, f32[8,8,128]{2,1,0:T(8,128)S(1)}, f32[8,128]{1,0:T(8,128)S(1)}) custom-call(f32[1024,512]{1,0:T(8,128)} %bitcast.5, bf16[1024,512]{1,0:T(8,128)(2,1)} %bitcast.6), custom_call_target="tpu_custom_call" | custom-call | tf_op jit(solution)/shard_map/local/pallas_call | solution.py:159
  2.7 0.0 copy-start
  2.7 27.7 %conditional.2 = ((f32[8,128]{1,0:T(8,128)S(1)}, f32[8,128]{1,0:T(8,128)S(1)}, f32[8,128]{1,0:T(8,128)S(1)})) conditional(s32[]{:T(128)} %convert_element_type.4, () %tuple.19, f32[8,128]{1,0:T(8,128)S(1)} %get-tuple-element.27), branch_computations={%region_0.0_spmd, %region_1.0_spmd} | conditional | bytes 397320 | solution.py:188
  2.7 27.6 %all_to_all.13.gathered = f32[32,8,128]{2,1,0:T(8,128)S(1)} all-to-all(f32[32,8,128]{2,1,0:T(8,128)S(1)} %broadcast_in_dim.8), channel_id=1, replica_groups={{0,8,16,24,32,40,48,56,64,72,80,88,96,104,112,120,128,136,144,152,160,1..., dimensions={0} | all-to-all | bytes 262144 | tf_op jit(solution)/shard_map/cond/branch_1_fun/all_to_all | solution.py:185
  30.4 0.1 prefix.2
  30.4 1.3 %collective-permute-start = (f32[8,128]{1,0:T(8,128)S(1)}, f32[8,128]{1,0:T(8,128)S(1)}, u32[]{:S(2)}, u32[]{:S(2)}) collective-permute-start(f32[8,128]{1,0:T(8,128)S(1)} %get-tuple-element.32), channel_id=1, source_target_pairs={{0,504},{8,496},{16,488},{24,480},{32,472},{40,464},{48,456},{56,4... | collective-permute-start | bytes 12296 | tf_op jit(solution)/shard_map/ppermute | solution.py:191
  31.8 0.7 %collective-permute-done.start = f32[8,128]{1,0:T(8,128)S(1)} collective-permute-done((f32[8,128]{1,0:T(8,128)S(1)}, f32[8,128]{1,0:T(8,128)S(1)}, u32[]{:S(2)}, u32[]{:S(2)}) %collective-permute-start) | collective-permute-done | bytes 4128 | tf_op jit(solution)/shard_map/ppermute | solution.py:191
  32.5 0.6 %carry.1 = (f32[1024,512]{1,0:T(8,128)S(1)}, f32[8,8,128]{2,1,0:T(8,128)S(1)}) custom-call(bf16[1024,512]{1,0:T(8,128)(2,1)S(1)} %get-tuple-element.24.drop, f32[1024,512]{1,0:T(8,128)S(1)} %get-tuple-element.25.inner, f32[8,8,128]{2,1,0:T(8,128)S(1)} %get-tuple-element.26.marks, f32[8,128]{1,0:T(8,128)S(1)} %get-tuple-element.30.keep, ...), custom_call_target="tpu_custom_call" | custom-call | tf_op jit(solution)/shard_map/carry/pallas_call | solution.py:195
  33.1 10.0 %all_to_all.15.powers = f32[8,8,128]{2,1,0:T(8,128)S(1)} all-to-all(f32[8,8,128]{2,1,0:T(8,128)S(1)} %get-tuple-element.34), channel_id=1, replica_groups=mesh['sp'=64,'tp'=8] {'tp'}, dimensions={0} | all-to-all | bytes 65536 | tf_op jit(solution)/shard_map/all_to_all | solution.py:203
  43.1 0.0 copy-done
  43.1 1.3 %norm.1 = bf16[1024,512]{1,0:T(8,128)(2,1)} custom-call(f32[1024,512]{1,0:T(8,128)S(1)} %get-tuple-element.33.forward, f32[8,8,128]{2,1,0:T(8,128)S(1)} %all_to_all.15.powers, f32[1,512]{1,0:T(1,128)S(1)} %bitcast.4), custom_call_target="tpu_custom_call" | custom-call | tf_op jit(solution)/shard_map/norm/pallas_call | solution.py:204
  (2 shorter events, 0.0 us)
Async XLA Ops:
  2.7 40.4 %copy-start = (f32[512]{0:T(512)S(1)}, f32[512]{0:T(512)}, u32[]{:S(2)}) copy-start(f32[512]{0:T(512)} %param.9) | copy-start | bytes 6148
  30.4 2.0 %collective-permute-start = (f32[8,128]{1,0:T(8,128)S(1)}, f32[8,128]{1,0:T(8,128)S(1)}, u32[]{:S(2)}, u32[]{:S(2)}) collective-permute-start(f32[8,128]{1,0:T(8,128)S(1)} %get-tuple-element.32), channel_id=1, source_target_pairs={{0,504},{8,496},{16,488},{24,480},{32,472},{40,464},{48,456},{56,4... | collective-permute-start | bytes 12296 | tf_op jit(solution)/shard_map/ppermute | solution.py:191

commit v4 on v3

--- a/solution.py
+++ b/solution.py
@@ -68,14 +68,14 @@
     message[...] = as_tile(kept, ended)
 
 
-def prefix_kernel(axis, gathered, keep, end, total):
+def prefix_kernel(axis, gathered, keep, end, *whole):
     peers, high, lanes = gathered.shape
     row = lax.broadcasted_iota(jnp.int32, (high, lanes), 0)
     before = jnp.where(row >= high // 2, lax.rem(lax.axis_index(axis), peers), 0)
-    counted = jnp.where(row >= high // 2, peers, 0)
-    own, whole = [], []
+    counts = [before] + [jnp.where(row >= high // 2, peers, 0)] * bool(whole)
+    found = [[] for _ in counts]
     for first in range(0, peers, 8):
-        for count, links in ((before, own), (counted, whole)):
+        for count, links in zip(counts, found):
             kept = ended = None
             for p in range(first, min(first + 8, peers)):
                 t = gathered[p]
@@ -84,24 +84,22 @@
                 ended = t if ended is None else ended * k + t
                 kept = k if kept is None else kept * k
             links.append((kept, ended))
-    kept, ended = own[0]
-    for k, e in own[1:]:
-        kept, ended = kept * k, ended * k + e
-    keep[...] = kept
-    end[...] = ended
-    ended = whole[0][1]
-    for k, e in whole[1:]:
-        ended = ended * k + e
-    total[...] = ended
-
-
-def carry_kernel(drop, inner, marks, keep, end, start, forward, message):
+    for links, out in zip(found, ((keep, end), whole)):
+        kept, ended = links[0]
+        for k, e in links[1:]:
+            kept, ended = kept * k, ended * k + e
+        for ref, value in zip(out[::-1], (ended, kept)):
+            ref[...] = value
+
+
+def carry_kernel(drop, inner, marks, keep, end, *rest):
+    *starts, forward, message = rest
     length, width = drop.shape
     blocks, _, lanes = marks.shape
     groups = width // lanes
     block = length // blocks
     row = lax.broadcasted_iota(jnp.int32, (8, lanes), 0)
-    state = start[...] * keep[...] + end[...]
+    state = sum(start[...] for start in starts) * keep[...] + end[...]
     ones = jnp.ones((8, lanes), BF16)
     out = jnp.zeros((8, lanes), F32)
     for b in range(blocks):
@@ -147,7 +145,7 @@
     total_length = length * stretches
     rate = LOG2E / total_length
     block, stage = LANES, 512
-    half = stretches // 2
+    half, quarter = stretches // 2, stretches // 4
     blocks = length // block
     limit = pltpu.CompilerParams(vmem_limit_bytes=24 * 1024 * 1024)
     wide = jax.ShapeDtypeStruct((length, width), F32)
@@ -169,37 +167,57 @@
         compiler_params=limit,
         name="local",
     )(*(pltpu.with_memory_space_constraint(a[0], pltpu.HBM) for a in (fade_rate, update_in)))
-    prefix = pl.pallas_call(
-        functools.partial(prefix_kernel, "sp"),
-        out_shape=(tile,) * 3,
-        in_specs=[VMEM],
-        out_specs=(VMEM,) * 3,
-        compiler_params=limit,
-        name="prefix",
-    )
-    early = lax.axis_index("sp") < half
-    halves = [list(range(half)), list(range(half, stretches))]
-
-    def within_half(summary):
-        copies = jnp.broadcast_to(summary, (half, *summary.shape))
-        gathered = lax.all_to_all(copies, "sp", 0, 0, axis_index_groups=halves, tiled=True)
-        return prefix(gathered)
-
-    keep, end, total = lax.cond(
-        early, within_half, lambda s: (jnp.zeros_like(s),) * 3, summary
-    )
-    start = lax.ppermute(total, "sp", [(i, stretches - 1 - i) for i in range(half)])
+    me = lax.axis_index("sp")
+
+    def within(size, whole):
+        groups = [list(range(at, at + size)) for at in range(0, stretches, size)]
+        prefix = pl.pallas_call(
+            functools.partial(prefix_kernel, "sp"),
+            out_shape=(tile,) * (2 + whole),
+            in_specs=[VMEM],
+            out_specs=(VMEM,) * (2 + whole),
+            compiler_params=limit,
+            name="prefix",
+        )
+
+        def found(summary, *_):
+            copies = jnp.broadcast_to(summary, (size, *summary.shape))
+            return prefix(
+                lax.all_to_all(copies, "sp", 0, 0, axis_index_groups=groups, tiled=True)
+            )
+
+        return found
+
+    none = jnp.zeros((8, LANES), F32)
+    keep, end, first = lax.cond(
+        me < quarter, within(quarter, 1), lambda *_: (none,) * 3, summary
+    )
+    handed = [lax.ppermute(first, "sp", [(i, i + quarter) for i in range(quarter)])]
+    keep, end, kept, ended = lax.cond(
+        me // quarter == 1,
+        within(quarter, 2),
+        lambda _, *found: (*found, none, none),
+        summary,
+        keep,
+        end,
+    )
+    second = handed[0] * kept + ended
+    for pairs in (
+        [(quarter + i, 2 * quarter + i) for i in range(quarter)],
+        [(quarter + i, 3 * quarter + (i + quarter // 2) % quarter) for i in range(quarter)],
+    ):
+        handed.append(lax.ppermute(second, "sp", pairs))
     keep, end = lax.cond(
-        early, lambda s, *found: found, lambda s, *_: within_half(s)[:2], summary, keep, end
+        me >= half, within(half, 0), lambda _, *found: found, summary, keep, end
     )
     forward, power = pl.pallas_call(
         carry_kernel,
         out_shape=(wide, tiles(parts)),
-        in_specs=[VMEM] * 6,
+        in_specs=[VMEM] * 8,
         out_specs=(VMEM, VMEM),
         compiler_params=limit,
         name="carry",
-    )(drop, inner, marks, keep, end, start)
+    )(drop, inner, marks, keep, end, *handed)
     powers = lax.all_to_all(power, "tp", 0, 0, tiled=True)
     out = pl.pallas_call(
         functools.partial(norm_kernel, width * parts, total_length),

time: 44.6 us -> 41.3 us (0.926)
  the two profiles are of different devices: /device:TPU:1 before, /device:TPU:256 now
where the time goes in v4:
time: 41.3 us; the launch traced here: 41.1 us
  blocking collectives  33.7 us (82%)
  Pallas kernels  4.62 us (11%)
  starting transfers between devices  2.62 us (6%)
    all_to_all x1, blocking collectives, found(): lax.all_to_all(copies, 'sp', 0, 0, axis_index_groups=groups, tiled=True)  25.3 us
    all_to_all x1, blocking collectives, per_device(): powers = lax.all_to_all(power, 'tp', 0, 0, tiled=True)  8.31 us
    pallas_call x1, Pallas kernels, per_device(): pl.pallas_call(functools.partial(local_kernel, block, stage, rate), out_s...  2.68 us
    ppermute x2, starting transfers between devices, per_device(): handed.append(lax.ppermute(second, 'sp', pairs))  1.95 us
    pallas_call x1, Pallas kernels, per_device(): pl.pallas_call(functools.partial(norm_kernel, width * parts, total_length...  1.29 us
  transfers between devices with their start and end apart: 3, of which 0 were waited for; matrix products, arithmetic and copies ran while one was open for 0% of the time, Pallas kernels for 0%

profile of v4, /device:TPU:256, one launch (start us, length us, event | category | flops | bytes accessed | tf_op | source)
XLA Modules:
  0.0 41.1 jit_solution(3382524721654613678)
XLA Ops:
  0.0 2.7 %local.1 = (bf16[1024,512]{1,0:T(8,128)(2,1)S(1)}, f32[1024,512]{1,0:T(8,128)S(1)}, f32[8,8,128]{2,1,0:T(8,128)S(1)}, f32[8,128]{1,0:T(8,128)S(1)}) custom-call(f32[1024,512]{1,0:T(8,128)} %bitcast.5, bf16[1024,512]{1,0:T(8,128)(2,1)} %bitcast.6), custom_call_target="tpu_custom_call" | custom-call | tf_op jit(solution)/shard_map/local/pallas_call | solution.py:157
  2.7 0.0 copy-start
  2.8 0.7 %collective-permute-start = (f32[8,128]{1,0:T(8,128)S(1)}, f32[8,128]{1,0:T(8,128)S(1)}, u32[]{:S(2)}, u32[]{:S(2)}) collective-permute-start(f32[8,128]{1,0:T(8,128)S(1)} %get-tuple-element.43), channel_id=1, source_target_pairs={{0,128},{8,136},{16,144},{24,152},{32,160},{40,168},{48,176},{56,1... | collective-permute-start | bytes 12296 | tf_op jit(solution)/shard_map/ppermute | solution.py:195
  3.5 0.0 collective-permute-done.rest_0_
  3.5 0.7 %collective-permute-start.2 = (f32[8,128]{1,0:T(8,128)S(1)}, f32[8,128]{1,0:T(8,128)S(1)}, u32[]{:S(2)}, u32[]{:S(2)}) collective-permute-start(f32[8,128]{1,0:T(8,128)S(1)} %multiply_add_fusion), channel_id=1, source_target_pairs={{128,448},{136,456},{144,464},{152,472},{160,480},{168,488},{176,4... | collective-permute-start | bytes 12296 | tf_op jit(solution)/shard_map/ppermute | solution.py:209
  4.2 1.3 %collective-permute-start.1 = (f32[8,128]{1,0:T(8,128)S(1)}, f32[8,128]{1,0:T(8,128)S(1)}, u32[]{:S(2)}, u32[]{:S(2)}) collective-permute-start(f32[8,128]{1,0:T(8,128)S(1)} %multiply_add_fusion), channel_id=1, source_target_pairs={{128,256},{136,264},{144,272},{152,280},{160,288},{168,296},{176,3... | collective-permute-start | bytes 12296 | tf_op jit(solution)/shard_map/ppermute | solution.py:209
  5.5 25.4 %conditional.5 = ((f32[8,128]{1,0:T(8,128)S(1)}, f32[8,128]{1,0:T(8,128)S(1)})) conditional(s32[]{:T(128)} %convert_element_type.9, (f32[8,128]{1,0:T(8,128)S(1)}, f32[8,128]{1,0:T(8,128)S(1)}) %tuple.27, f32[8,128]{1,0:T(8,128)S(1)} %get-tuple-element.36), branch_computations={%region_4.5_spmd, %region_5.6_spmd} | conditional | bytes 397320 | solution.py:210
  5.5 25.3 %all_to_all.19.gathered = f32[32,8,128]{2,1,0:T(8,128)S(1)} all-to-all(f32[32,8,128]{2,1,0:T(8,128)S(1)} %broadcast_in_dim.18), channel_id=1, replica_groups={{0,8,16,24,32,40,48,56,64,72,80,88,96,104,112,120,128,136,144,152,160,1..., dimensions={0} | all-to-all | bytes 262144 | tf_op jit(solution)/shard_map/cond/branch_1_fun/all_to_all | solution.py:186
  30.9 0.0 collective-permute-done.2.rest_2_
  30.9 0.0 collective-permute-done.1.rest_1_
  30.9 0.6 %carry.1 = (f32[1024,512]{1,0:T(8,128)S(1)}, f32[8,8,128]{2,1,0:T(8,128)S(1)}) custom-call(bf16[1024,512]{1,0:T(8,128)(2,1)S(1)} %get-tuple-element.33.drop, f32[1024,512]{1,0:T(8,128)S(1)} %get-tuple-element.34.inner, f32[8,8,128]{2,1,0:T(8,128)S(1)} %get-tuple-element.35.marks, f32[8,128]{1,0:T(8,128)S(1)} %get-tuple-element.41.keep, ...), custom_call_target="tpu_custom_call" | custom-call | tf_op jit(solution)/shard_map/carry/pallas_call | solution.py:213
  31.5 8.3 %all_to_all.20.powers = f32[8,8,128]{2,1,0:T(8,128)S(1)} all-to-all(f32[8,8,128]{2,1,0:T(8,128)S(1)} %get-tuple-element.47), channel_id=1, replica_groups=mesh['sp'=64,'tp'=8] {'tp'}, dimensions={0} | all-to-all | bytes 65536 | tf_op jit(solution)/shard_map/all_to_all | solution.py:221
  39.8 0.0 copy-done
  39.8 1.3 %norm.1 = bf16[1024,512]{1,0:T(8,128)(2,1)} custom-call(f32[1024,512]{1,0:T(8,128)S(1)} %get-tuple-element.46.forward, f32[8,8,128]{2,1,0:T(8,128)S(1)} %all_to_all.20.powers, f32[1,512]{1,0:T(1,128)S(1)} %bitcast.4), custom_call_target="tpu_custom_call" | custom-call | tf_op jit(solution)/shard_map/norm/pallas_call | solution.py:222
  (10 shorter events, 0.1 us)
Async XLA Ops:
  2.7 37.1 %copy-start = (f32[512]{0:T(512)S(1)}, f32[512]{0:T(512)}, u32[]{:S(2)}) copy-start(f32[512]{0:T(512)} %param.11) | copy-start | bytes 6148
  2.8 0.7 %collective-permute-start = (f32[8,128]{1,0:T(8,128)S(1)}, f32[8,128]{1,0:T(8,128)S(1)}, u32[]{:S(2)}, u32[]{:S(2)}) collective-permute-start(f32[8,128]{1,0:T(8,128)S(1)} %get-tuple-element.43), channel_id=1, source_target_pairs={{0,128},{8,136},{16,144},{24,152},{32,160},{40,168},{48,176},{56,1... | collective-permute-start | bytes 12296 | tf_op jit(solution)/shard_map/ppermute | solution.py:195
  3.5 27.4 %collective-permute-start.2 = (f32[8,128]{1,0:T(8,128)S(1)}, f32[8,128]{1,0:T(8,128)S(1)}, u32[]{:S(2)}, u32[]{:S(2)}) collective-permute-start(f32[8,128]{1,0:T(8,128)S(1)} %multiply_add_fusion), channel_id=1, source_target_pairs={{128,448},{136,456},{144,464},{152,472},{160,480},{168,488},{176,4... | collective-permute-start | bytes 12296 | tf_op jit(solution)/shard_map/ppermute | solution.py:209
  4.2 26.7 %collective-permute-start.1 = (f32[8,128]{1,0:T(8,128)S(1)}, f32[8,128]{1,0:T(8,128)S(1)}, u32[]{:S(2)}, u32[]{:S(2)}) collective-permute-start(f32[8,128]{1,0:T(8,128)S(1)} %multiply_add_fusion), channel_id=1, source_target_pairs={{128,256},{136,264},{144,272},{152,280},{160,288},{168,296},{176,3... | collective-permute-start | bytes 12296 | tf_op jit(solution)/shard_map/ppermute | solution.py:209

commit v5 on v4

--- a/solution.py
+++ b/solution.py
@@ -68,10 +68,11 @@
     message[...] = as_tile(kept, ended)
 
 
-def prefix_kernel(axis, gathered, keep, end, *whole):
+def prefix_kernel(axis, split, gathered, *outs):
     peers, high, lanes = gathered.shape
     row = lax.broadcasted_iota(jnp.int32, (high, lanes), 0)
     before = jnp.where(row >= high // 2, lax.rem(lax.axis_index(axis), peers), 0)
+    own, whole = outs[:split], outs[split:]
     counts = [before] + [jnp.where(row >= high // 2, peers, 0)] * bool(whole)
     found = [[] for _ in counts]
     for first in range(0, peers, 8):
@@ -84,7 +85,7 @@
                 ended = t if ended is None else ended * k + t
                 kept = k if kept is None else kept * k
             links.append((kept, ended))
-    for links, out in zip(found, ((keep, end), whole)):
+    for links, out in zip(found, (own, whole)):
         kept, ended = links[0]
         for k, e in links[1:]:
             kept, ended = kept * k, ended * k + e
@@ -92,14 +93,13 @@
             ref[...] = value
 
 
-def carry_kernel(drop, inner, marks, keep, end, *rest):
-    *starts, forward, message = rest
+def carry_kernel(drop, inner, marks, start, forward, message):
     length, width = drop.shape
     blocks, _, lanes = marks.shape
     groups = width // lanes
     block = length // blocks
     row = lax.broadcasted_iota(jnp.int32, (8, lanes), 0)
-    state = sum(start[...] for start in starts) * keep[...] + end[...]
+    state = start[...]
     ones = jnp.ones((8, lanes), BF16)
     out = jnp.zeros((8, lanes), F32)
     for b in range(blocks):
@@ -169,13 +169,13 @@
     )(*(pltpu.with_memory_space_constraint(a[0], pltpu.HBM) for a in (fade_rate, update_in)))
     me = lax.axis_index("sp")
 
-    def within(size, whole):
+    def within(size, own, whole):
         groups = [list(range(at, at + size)) for at in range(0, stretches, size)]
         prefix = pl.pallas_call(
-            functools.partial(prefix_kernel, "sp"),
-            out_shape=(tile,) * (2 + whole),
+            functools.partial(prefix_kernel, "sp", own),
+            out_shape=(tile,) * (own + whole),
             in_specs=[VMEM],
-            out_specs=(VMEM,) * (2 + whole),
+            out_specs=(VMEM,) * (own + whole),
             compiler_params=limit,
             name="prefix",
         )
@@ -188,36 +188,46 @@
 
         return found
 
-    none = jnp.zeros((8, LANES), F32)
-    keep, end, first = lax.cond(
-        me < quarter, within(quarter, 1), lambda *_: (none,) * 3, summary
+    def early_half(summary):
+        end, first = lax.cond(
+            me < quarter, within(quarter, 1, 1), lambda s: (s, s), summary
+        )
+        start = lax.ppermute(first, "sp", [(i, i + quarter) for i in range(quarter)])
+        keep, end, kept, ended = lax.cond(
+            me < quarter,
+            lambda s, end: (s, end, s, s),
+            within(quarter, 2, 2),
+            summary,
+            end,
+        )
+        return start * keep + end, start * kept + ended
+
+    def after_first_quarter(summary, state, second):
+        start = sum(
+            lax.ppermute(second, "sp", pairs)
+            for pairs in (
+                [(quarter + i, 2 * quarter + i) for i in range(quarter)],
+                [(quarter + i, 3 * quarter + (i + quarter // 2) % quarter) for i in range(quarter)],
+            )
+        )
+        keep, end = lax.cond(
+            me < half, lambda summary, state: (summary, state), within(half, 2, 0), summary, state
+        )
+        return start * keep + end
+
+    state, second = lax.cond(me < half, early_half, lambda s: (s, s), summary)
+    state = lax.cond(
+        me < quarter, lambda _, state, *__: state, after_first_quarter, summary, state, second
     )
-    handed = [lax.ppermute(first, "sp", [(i, i + quarter) for i in range(quarter)])]
-    keep, end, kept, ended = lax.cond(
-        me // quarter == 1,
-        within(quarter, 2),
-        lambda _, *found: (*found, none, none),
-        summary,
-        keep,
-        end,
-    )
-    second = handed[0] * kept + ended
-    for pairs in (
-        [(quarter + i, 2 * quarter + i) for i in range(quarter)],
-        [(quarter + i, 3 * quarter + (i + quarter // 2) % quarter) for i in range(quarter)],
-    ):
-        handed.append(lax.ppermute(second, "sp", pairs))
-    keep, end = lax.cond(
-        me >= half, within(half, 0), lambda _, *found: found, summary, keep, end
-    )
+    state = pltpu.with_memory_space_constraint(state, pltpu.VMEM)
     forward, power = pl.pallas_call(
         carry_kernel,
         out_shape=(wide, tiles(parts)),
-        in_specs=[VMEM] * 8,
+        in_specs=[VMEM] * 4,
         out_specs=(VMEM, VMEM),
         compiler_params=limit,
         name="carry",
-    )(drop, inner, marks, keep, end, *handed)
+    )(drop, inner, marks, state)
     powers = lax.all_to_all(power, "tp", 0, 0, tiled=True)
     out = pl.pallas_call(
         functools.partial(norm_kernel, width * parts, total_length),

time: 41.3 us -> 41 us (level)
  the two profiles are of different devices: /device:TPU:256 before, /device:TPU:128 now
where the time goes in v5:
time: 41 us; the launch traced here: 40.8 us
  blocking collectives  30.6 us (75%)
  Pallas kernels  4.61 us (11%)
  starting transfers between devices  3.86 us (9%)
  waiting for transfers between devices  1.54 us (4%)
    all_to_all x1, blocking collectives, found(): lax.all_to_all(copies, 'sp', 0, 0, axis_index_groups=groups, tiled=True)  22.5 us
    all_to_all x1, blocking collectives, per_device(): powers = lax.all_to_all(power, 'tp', 0, 0, tiled=True)  8.12 us
    pallas_call x1, Pallas kernels, per_device(): pl.pallas_call(functools.partial(local_kernel, block, stage, rate), out_s...  2.69 us
    ppermute x2, starting transfers between devices, after_first_quarter(): lax.ppermute(second, 'sp', pairs)  2.57 us
    ppermute x1, starting transfers between devices, early_half(): lax.ppermute(first, 'sp', [(i, i + quarter) for i in range(quarter)])  1.29 us
    pallas_call x1, Pallas kernels, per_device(): pl.pallas_call(functools.partial(norm_kernel, width * parts, total_length...  1.29 us
    ppermute x2, waiting for transfers between devices, after_first_quarter(): lax.ppermute(second, 'sp', pairs)  1.28 us
  transfers between devices with their start and end apart: 3, of which 2 were waited for; matrix products, arithmetic and copies ran while one was open for 0% of the time, Pallas kernels for 0%

profile of v5, /device:TPU:128, one launch (start us, length us, event | category | flops | bytes accessed | tf_op | source)
XLA Modules:
  0.0 40.8 jit_solution(18443857865872373950)
XLA Ops:
  0.0 2.7 %local.1 = (bf16[1024,512]{1,0:T(8,128)(2,1)S(1)}, f32[1024,512]{1,0:T(8,128)S(1)}, f32[8,8,128]{2,1,0:T(8,128)S(1)}, f32[8,128]{1,0:T(8,128)S(1)}) custom-call(f32[1024,512]{1,0:T(8,128)} %bitcast.5, bf16[1024,512]{1,0:T(8,128)(2,1)} %bitcast.6), custom_call_target="tpu_custom_call" | custom-call | tf_op jit(solution)/shard_map/local/pallas_call | solution.py:157
  2.7 0.0 copy-start
  2.7 24.2 %conditional.5 = (f32[8,128]{1,0:T(8,128)S(1)}, f32[8,128]{1,0:T(8,128)S(1)}) conditional(s32[]{:T(128)} %convert_element_type.14, f32[8,128]{1,0:T(8,128)S(1)} %get-tuple-element.61, (s32[]{:T(128)}, f32[8,128]{1,0:T(8,128)S(1)}) %tuple.39), branch_computations={%region_0.0_spmd, %region_1.0_spmd} | conditional | flops 4098 | bytes 446566 | solution.py:218
  2.8 1.3 %collective-permute-start = (f32[8,128]{1,0:T(8,128)S(1)}, f32[8,128]{1,0:T(8,128)S(1)}, u32[]{:S(2)}, u32[]{:S(2)}) collective-permute-start(f32[8,128]{1,0:T(8,128)S(1)} %get-tuple-element.38), channel_id=1, source_target_pairs={{0,128},{8,136},{16,144},{24,152},{32,160},{40,168},{48,176},{56,1... | collective-permute-start | bytes 12296 | tf_op jit(solution)/shard_map/cond/branch_1_fun/ppermute | solution.py:195
  4.1 22.6 %conditional.1 = ((f32[8,128]{1,0:T(8,128)S(1)}, f32[8,128]{1,0:T(8,128)S(1)}, f32[8,128]{1,0:T(8,128)S(1)}, f32[8,128]{1,0:T(8,128)S(1)})) conditional(s32[]{:T(128)} %convert_element_type.2, f32[8,128]{1,0:T(8,128)S(1)} %get-tuple-element.37, (f32[8,128]{1,0:T(8,128)S(1)}, f32[8,128]{1,0:T(8,128)S(1)}) %tuple.34), branch_computations={%region_4.0_spmd, %region_5.0_spmd} | conditional | bytes 200712 | solution.py:196
  4.1 22.5 %all_to_all.18.gathered = f32[16,8,128]{2,1,0:T(8,128)S(1)} all-to-all(f32[16,8,128]{2,1,0:T(8,128)S(1)} %broadcast_in_dim.11), channel_id=1, replica_groups={{0,8,16,24,32,40,48,56,64,72,80,88,96,104,112,120},{128,136,144,152,160..., dimensions={0} | all-to-all | bytes 131072 | tf_op jit(solution)/shard_map/cond/branch_1_fun/cond/branch_0_fun/all_to_all | solution.py:186
  26.7 0.3 collective-permute-done
  26.9 3.9 %conditional.6 = (f32[8,128]{1,0:T(8,128)S(1)}) conditional(s32[]{:T(128)} %convert_element_type.13, (f32[8,128]{1,0:T(8,128)S(1)}, s32[]{:T(128)}, f32[8,128]{1,0:T(8,128)S(1)}, f32[8,128]{1,0:T(8,128)S(1)}) %tuple.40, f32[8,128]{1,0:T(8,128)S(1)} %get-tuple-element.63), branch_computations={%region_6.0_spmd, %region_9.0_spmd} | conditional | flops 3074 | bytes 450686 | solution.py:219
  26.9 1.3 %collective-permute-start.2 = (f32[8,128]{1,0:T(8,128)S(1)}, f32[8,128]{1,0:T(8,128)S(1)}, u32[]{:S(2)}, u32[]{:S(2)}) collective-permute-start(f32[8,128]{1,0:T(8,128)S(1)} %get-tuple-element.44), channel_id=1, source_target_pairs={{128,448},{136,456},{144,464},{152,472},{160,480},{168,488},{176,4... | collective-permute-start | bytes 12296 | tf_op jit(solution)/shard_map/cond/branch_0_fun/ppermute | solution.py:207
  28.2 1.3 %collective-permute-start.1 = (f32[8,128]{1,0:T(8,128)S(1)}, f32[8,128]{1,0:T(8,128)S(1)}, u32[]{:S(2)}, u32[]{:S(2)}) collective-permute-start(f32[8,128]{1,0:T(8,128)S(1)} %get-tuple-element.44), channel_id=1, source_target_pairs={{128,256},{136,264},{144,272},{152,280},{160,288},{168,296},{176,3... | collective-permute-start | bytes 12296 | tf_op jit(solution)/shard_map/cond/branch_0_fun/ppermute | solution.py:207
  29.5 0.0 collective-permute-done.2
  29.5 1.3 %collective-permute-done.1 = f32[8,128]{1,0:T(8,128)S(1)} collective-permute-done((f32[8,128]{1,0:T(8,128)S(1)}, f32[8,128]{1,0:T(8,128)S(1)}, u32[]{:S(2)}, u32[]{:S(2)}) %collective-permute-start.1) | collective-permute-done | bytes 4128 | tf_op jit(solution)/shard_map/cond/branch_0_fun/ppermute | solution.py:207
  30.8 0.6 %carry.1 = (f32[1024,512]{1,0:T(8,128)S(1)}, f32[8,8,128]{2,1,0:T(8,128)S(1)}) custom-call(bf16[1024,512]{1,0:T(8,128)(2,1)S(1)} %get-tuple-element.58.drop, f32[1024,512]{1,0:T(8,128)S(1)} %get-tuple-element.59.inner, f32[8,8,128]{2,1,0:T(8,128)S(1)} %get-tuple-element.60.marks, f32[8,128]{1,0:T(8,128)S(1)} %get-tuple-element.91.start), custom_call_target="tpu_custom_call" | custom-call | tf_op jit(solution)/shard_map/carry/pallas_call | solution.py:223
  31.4 8.1 %all_to_all.20.powers = f32[8,8,128]{2,1,0:T(8,128)S(1)} all-to-all(f32[8,8,128]{2,1,0:T(8,128)S(1)} %get-tuple-element.65), channel_id=1, replica_groups=mesh['sp'=64,'tp'=8] {'tp'}, dimensions={0} | all-to-all | bytes 65536 | tf_op jit(solution)/shard_map/all_to_all | solution.py:231
  39.5 0.0 copy-done
  39.5 1.3 %norm.1 = bf16[1024,512]{1,0:T(8,128)(2,1)} custom-call(f32[1024,512]{1,0:T(8,128)S(1)} %get-tuple-element.64.forward, f32[8,8,128]{2,1,0:T(8,128)S(1)} %all_to_all.20.powers, f32[1,512]{1,0:T(1,128)S(1)} %bitcast.4), custom_call_target="tpu_custom_call" | custom-call | tf_op jit(solution)/shard_map/norm/pallas_call | solution.py:232
  (8 shorter events, 0.1 us)
Async XLA Ops:
  2.7 36.8 %copy-start = (f32[512]{0:T(512)S(1)}, f32[512]{0:T(512)}, u32[]{:S(2)}) copy-start(f32[512]{0:T(512)} %param.15) | copy-start | bytes 6148
  2.8 24.1 %collective-permute-start = (f32[8,128]{1,0:T(8,128)S(1)}, f32[8,128]{1,0:T(8,128)S(1)}, u32[]{:S(2)}, u32[]{:S(2)}) collective-permute-start(f32[8,128]{1,0:T(8,128)S(1)} %get-tuple-element.38), channel_id=1, source_target_pairs={{0,128},{8,136},{16,144},{24,152},{32,160},{40,168},{48,176},{56,1... | collective-permute-start | bytes 12296 | tf_op jit(solution)/shard_map/cond/branch_1_fun/ppermute | solution.py:195
  26.9 2.6 %collective-permute-start.2 = (f32[8,128]{1,0:T(8,128)S(1)}, f32[8,128]{1,0:T(8,128)S(1)}, u32[]{:S(2)}, u32[]{:S(2)}) collective-permute-start(f32[8,128]{1,0:T(8,128)S(1)} %get-tuple-element.44), channel_id=1, source_target_pairs={{128,448},{136,456},{144,464},{152,472},{160,480},{168,488},{176,4... | collective-permute-start | bytes 12296 | tf_op jit(solution)/shard_map/cond/branch_0_fun/ppermute | solution.py:207
  28.2 2.6 %collective-permute-start.1 = (f32[8,128]{1,0:T(8,128)S(1)}, f32[8,128]{1,0:T(8,128)S(1)}, u32[]{:S(2)}, u32[]{:S(2)}) collective-permute-start(f32[8,128]{1,0:T(8,128)S(1)} %get-tuple-element.44), channel_id=1, source_target_pairs={{128,256},{136,264},{144,272},{152,280},{160,288},{168,296},{176,3... | collective-permute-start | bytes 12296 | tf_op jit(solution)/shard_map/cond/branch_0_fun/ppermute | solution.py:207

commit v6 on v5

--- a/solution.py
+++ b/solution.py
@@ -192,7 +192,7 @@
         end, first = lax.cond(
             me < quarter, within(quarter, 1, 1), lambda s: (s, s), summary
         )
-        start = lax.ppermute(first, "sp", [(i, i + quarter) for i in range(quarter)])
+        start = lax.ppermute(first, "sp", [(i, quarter + (i + quarter // 2) % quarter) for i in range(quarter)])
         keep, end, kept, ended = lax.cond(
             me < quarter,
             lambda s, end: (s, end, s, s),

time: 41 us -> 40.8 us (level)
  transfers between devices with their start and end apart: 3 -> 3, of which waited for: 2 -> 1; matrix products, arithmetic and copies ran while one was open for 0% -> 0% of each run, Pallas kernels for 0% -> 0%
where the time goes in v6:
time: 40.8 us; the launch traced here: 40.6 us
  blocking collectives  30.6 us (75%)
  Pallas kernels  4.61 us (11%)
  starting transfers between devices  3.87 us (9%)
  waiting for transfers between devices  1.28 us (3%)
    all_to_all x1, blocking collectives, found(): lax.all_to_all(copies, 'sp', 0, 0, axis_index_groups=groups, tiled=True)  22.5 us
    all_to_all x1, blocking collectives, per_device(): powers = lax.all_to_all(power, 'tp', 0, 0, tiled=True)  8.12 us
    pallas_call x1, Pallas kernels, per_device(): pl.pallas_call(functools.partial(local_kernel, block, stage, rate), out_s...  2.69 us
    ppermute x2, starting transfers between devices, after_first_quarter(): lax.ppermute(second, 'sp', pairs)  2.58 us
    ppermute x1, starting transfers between devices, early_half(): lax.ppermute(first, 'sp', [(i, quarter + (i + quarter // 2) % quarter) fo...  1.29 us
    pallas_call x1, Pallas kernels, per_device(): pl.pallas_call(functools.partial(norm_kernel, width * parts, total_length...  1.29 us
    ppermute x2, waiting for transfers between devices, after_first_quarter(): lax.ppermute(second, 'sp', pairs)  1.28 us
  transfers between devices with their start and end apart: 3, of which 1 were waited for; matrix products, arithmetic and copies ran while one was open for 0% of the time, Pallas kernels for 0%

profile of v6, /device:TPU:128, one launch (start us, length us, event | category | flops | bytes accessed | tf_op | source)
XLA Modules:
  0.0 40.6 jit_solution(8987564914480067233)
XLA Ops:
  0.0 2.7 %local.1 = (bf16[1024,512]{1,0:T(8,128)(2,1)S(1)}, f32[1024,512]{1,0:T(8,128)S(1)}, f32[8,8,128]{2,1,0:T(8,128)S(1)}, f32[8,128]{1,0:T(8,128)S(1)}) custom-call(f32[1024,512]{1,0:T(8,128)} %bitcast.5, bf16[1024,512]{1,0:T(8,128)(2,1)} %bitcast.6), custom_call_target="tpu_custom_call" | custom-call | tf_op jit(solution)/shard_map/local/pallas_call | solution.py:157
  2.7 0.0 copy-start
  2.7 24.0 %conditional.5 = (f32[8,128]{1,0:T(8,128)S(1)}, f32[8,128]{1,0:T(8,128)S(1)}) conditional(s32[]{:T(128)} %convert_element_type.14, f32[8,128]{1,0:T(8,128)S(1)} %get-tuple-element.61, (s32[]{:T(128)}, f32[8,128]{1,0:T(8,128)S(1)}) %tuple.39), branch_computations={%region_0.0_spmd, %region_1.0_spmd} | conditional | flops 4098 | bytes 446566 | solution.py:218
  2.8 1.3 %collective-permute-start = (f32[8,128]{1,0:T(8,128)S(1)}, f32[8,128]{1,0:T(8,128)S(1)}, u32[]{:S(2)}, u32[]{:S(2)}) collective-permute-start(f32[8,128]{1,0:T(8,128)S(1)} %get-tuple-element.38), channel_id=1, source_target_pairs={{0,192},{8,200},{16,208},{24,216},{32,224},{40,232},{48,240},{56,2... | collective-permute-start | bytes 12296 | tf_op jit(solution)/shard_map/cond/branch_1_fun/ppermute | solution.py:195
  4.1 22.6 %conditional.1 = ((f32[8,128]{1,0:T(8,128)S(1)}, f32[8,128]{1,0:T(8,128)S(1)}, f32[8,128]{1,0:T(8,128)S(1)}, f32[8,128]{1,0:T(8,128)S(1)})) conditional(s32[]{:T(128)} %convert_element_type.2, f32[8,128]{1,0:T(8,128)S(1)} %get-tuple-element.37, (f32[8,128]{1,0:T(8,128)S(1)}, f32[8,128]{1,0:T(8,128)S(1)}) %tuple.34), branch_computations={%region_4.0_spmd, %region_5.0_spmd} | conditional | bytes 200712 | solution.py:196
  4.1 22.5 %all_to_all.18.gathered = f32[16,8,128]{2,1,0:T(8,128)S(1)} all-to-all(f32[16,8,128]{2,1,0:T(8,128)S(1)} %broadcast_in_dim.11), channel_id=1, replica_groups={{0,8,16,24,32,40,48,56,64,72,80,88,96,104,112,120},{128,136,144,152,160..., dimensions={0} | all-to-all | bytes 131072 | tf_op jit(solution)/shard_map/cond/branch_1_fun/cond/branch_0_fun/all_to_all | solution.py:186
  26.7 0.0 collective-permute-done
  26.7 3.9 %conditional.6 = (f32[8,128]{1,0:T(8,128)S(1)}) conditional(s32[]{:T(128)} %convert_element_type.13, (f32[8,128]{1,0:T(8,128)S(1)}, s32[]{:T(128)}, f32[8,128]{1,0:T(8,128)S(1)}, f32[8,128]{1,0:T(8,128)S(1)}) %tuple.40, f32[8,128]{1,0:T(8,128)S(1)} %get-tuple-element.63), branch_computations={%region_6.0_spmd, %region_9.0_spmd} | conditional | flops 3074 | bytes 450686 | solution.py:219
  26.7 1.3 %collective-permute-start.2 = (f32[8,128]{1,0:T(8,128)S(1)}, f32[8,128]{1,0:T(8,128)S(1)}, u32[]{:S(2)}, u32[]{:S(2)}) collective-permute-start(f32[8,128]{1,0:T(8,128)S(1)} %get-tuple-element.44), channel_id=1, source_target_pairs={{128,448},{136,456},{144,464},{152,472},{160,480},{168,488},{176,4... | collective-permute-start | bytes 12296 | tf_op jit(solution)/shard_map/cond/branch_0_fun/ppermute | solution.py:207
  28.0 1.3 %collective-permute-start.1 = (f32[8,128]{1,0:T(8,128)S(1)}, f32[8,128]{1,0:T(8,128)S(1)}, u32[]{:S(2)}, u32[]{:S(2)}) collective-permute-start(f32[8,128]{1,0:T(8,128)S(1)} %get-tuple-element.44), channel_id=1, source_target_pairs={{128,256},{136,264},{144,272},{152,280},{160,288},{168,296},{176,3... | collective-permute-start | bytes 12296 | tf_op jit(solution)/shard_map/cond/branch_0_fun/ppermute | solution.py:207
  29.3 0.0 collective-permute-done.2
  29.3 1.3 %collective-permute-done.1 = f32[8,128]{1,0:T(8,128)S(1)} collective-permute-done((f32[8,128]{1,0:T(8,128)S(1)}, f32[8,128]{1,0:T(8,128)S(1)}, u32[]{:S(2)}, u32[]{:S(2)}) %collective-permute-start.1) | collective-permute-done | bytes 4128 | tf_op jit(solution)/shard_map/cond/branch_0_fun/ppermute | solution.py:207
  30.6 0.6 %carry.1 = (f32[1024,512]{1,0:T(8,128)S(1)}, f32[8,8,128]{2,1,0:T(8,128)S(1)}) custom-call(bf16[1024,512]{1,0:T(8,128)(2,1)S(1)} %get-tuple-element.58.drop, f32[1024,512]{1,0:T(8,128)S(1)} %get-tuple-element.59.inner, f32[8,8,128]{2,1,0:T(8,128)S(1)} %get-tuple-element.60.marks, f32[8,128]{1,0:T(8,128)S(1)} %get-tuple-element.91.start), custom_call_target="tpu_custom_call" | custom-call | tf_op jit(solution)/shard_map/carry/pallas_call | solution.py:223
  31.2 8.1 %all_to_all.20.powers = f32[8,8,128]{2,1,0:T(8,128)S(1)} all-to-all(f32[8,8,128]{2,1,0:T(8,128)S(1)} %get-tuple-element.65), channel_id=1, replica_groups=mesh['sp'=64,'tp'=8] {'tp'}, dimensions={0} | all-to-all | bytes 65536 | tf_op jit(solution)/shard_map/all_to_all | solution.py:231
  39.3 0.0 copy-done
  39.3 1.3 %norm.1 = bf16[1024,512]{1,0:T(8,128)(2,1)} custom-call(f32[1024,512]{1,0:T(8,128)S(1)} %get-tuple-element.64.forward, f32[8,8,128]{2,1,0:T(8,128)S(1)} %all_to_all.20.powers, f32[1,512]{1,0:T(1,128)S(1)} %bitcast.4), custom_call_target="tpu_custom_call" | custom-call | tf_op jit(solution)/shard_map/norm/pallas_call | solution.py:232
  (8 shorter events, 0.1 us)
Async XLA Ops:
  2.7 36.6 %copy-start = (f32[512]{0:T(512)S(1)}, f32[512]{0:T(512)}, u32[]{:S(2)}) copy-start(f32[512]{0:T(512)} %param.15) | copy-start | bytes 6148
  2.8 23.9 %collective-permute-start = (f32[8,128]{1,0:T(8,128)S(1)}, f32[8,128]{1,0:T(8,128)S(1)}, u32[]{:S(2)}, u32[]{:S(2)}) collective-permute-start(f32[8,128]{1,0:T(8,128)S(1)} %get-tuple-element.38), channel_id=1, source_target_pairs={{0,192},{8,200},{16,208},{24,216},{32,224},{40,232},{48,240},{56,2... | collective-permute-start | bytes 12296 | tf_op jit(solution)/shard_map/cond/branch_1_fun/ppermute | solution.py:195
  26.7 2.6 %collective-permute-start.2 = (f32[8,128]{1,0:T(8,128)S(1)}, f32[8,128]{1,0:T(8,128)S(1)}, u32[]{:S(2)}, u32[]{:S(2)}) collective-permute-start(f32[8,128]{1,0:T(8,128)S(1)} %get-tuple-element.44), channel_id=1, source_target_pairs={{128,448},{136,456},{144,464},{152,472},{160,480},{168,488},{176,4... | collective-permute-start | bytes 12296 | tf_op jit(solution)/shard_map/cond/branch_0_fun/ppermute | solution.py:207
  28.0 2.6 %collective-permute-start.1 = (f32[8,128]{1,0:T(8,128)S(1)}, f32[8,128]{1,0:T(8,128)S(1)}, u32[]{:S(2)}, u32[]{:S(2)}) collective-permute-start(f32[8,128]{1,0:T(8,128)S(1)} %get-tuple-element.44), channel_id=1, source_target_pairs={{128,256},{136,264},{144,272},{152,280},{160,288},{168,296},{176,3... | collective-permute-start | bytes 12296 | tf_op jit(solution)/shard_map/cond/branch_0_fun/ppermute | solution.py:207

commit v7 on v6

--- a/solution.py
+++ b/solution.py
@@ -25,12 +25,12 @@
     return jnp.concatenate(lines, axis=0)
 
 
-def local_kernel(block, stage, rate, fade, update, drop, inner, marks, message, fades, updates, sems):
+def local_kernel(block, stages, rate, fade, update, drop, inner, marks, message, fades, updates, sems):
     length, width = fade.shape
     half = 2 * LANES
     copies = []
-    for b in range(length // stage):
-        rows = pl.ds(b * stage, stage)
+    for b, (at, to) in enumerate(zip(stages, (*stages[1:], length))):
+        rows = pl.ds(at, to - at)
         pair = (
             pltpu.make_async_copy(fade.at[rows], fades.at[rows], sems.at[0, b]),
             pltpu.make_async_copy(update.at[rows], updates.at[rows], sems.at[1, b]),
@@ -46,8 +46,8 @@
     kept, ended = None, None
     for b in range(length // block):
         rows = pl.ds(b * block, block)
-        if b * block % stage == 0:
-            for copy in copies[b * block // stage]:
+        if b * block in stages:
+            for copy in copies[stages.index(b * block)]:
                 copy.wait()
         keeps, ends = [], []
         for h in range(width // half):
@@ -144,7 +144,7 @@
     stretches, parts = lax.axis_size("sp"), lax.axis_size("tp")
     total_length = length * stretches
     rate = LOG2E / total_length
-    block, stage = LANES, 512
+    block, stages = LANES, (0, 384)
     half, quarter = stretches // 2, stretches // 4
     blocks = length // block
     limit = pltpu.CompilerParams(vmem_limit_bytes=24 * 1024 * 1024)
@@ -155,14 +155,14 @@
 
     tile = jax.ShapeDtypeStruct((8, LANES), F32)
     drop, inner, marks, summary = pl.pallas_call(
-        functools.partial(local_kernel, block, stage, rate),
+        functools.partial(local_kernel, block, stages, rate),
         out_shape=(jax.ShapeDtypeStruct((length, width), BF16), wide, tiles(blocks), tile),
         in_specs=[HBM, HBM],
         out_specs=(VMEM,) * 4,
         scratch_shapes=[
             pltpu.VMEM((length, width), F32),
             pltpu.VMEM((length, width), BF16),
-            pltpu.SemaphoreType.DMA((2, length // stage)),
+            pltpu.SemaphoreType.DMA((2, len(stages))),
         ],
         compiler_params=limit,
         name="local",
@@ -206,7 +206,7 @@
         start = sum(
             lax.ppermute(second, "sp", pairs)
             for pairs in (
-                [(quarter + i, 2 * quarter + i) for i in range(quarter)],
+                [(quarter + i, 2 * quarter + (i + quarter // 2) % quarter) for i in range(quarter)],
                 [(quarter + i, 3 * quarter + (i + quarter // 2) % quarter) for i in range(quarter)],
             )
         )

time: 40.8 us -> 40.8 us (level)
  no operation moved by 1% of the time
where the time goes in v7:
time: 40.8 us; the launch traced here: 40.6 us
  blocking collectives  30.6 us (75%)
  Pallas kernels  4.56 us (11%)
  starting transfers between devices  3.87 us (9%)
  waiting for transfers between devices  1.28 us (3%)
    all_to_all x1, blocking collectives, found(): lax.all_to_all(copies, 'sp', 0, 0, axis_index_groups=groups, tiled=True)  22.5 us
    all_to_all x1, blocking collectives, per_device(): powers = lax.all_to_all(power, 'tp', 0, 0, tiled=True)  8.12 us
    pallas_call x1, Pallas kernels, per_device(): pl.pallas_call(functools.partial(local_kernel, block, stages, rate), out_...  2.64 us
    ppermute x2, starting transfers between devices, after_first_quarter(): lax.ppermute(second, 'sp', pairs)  2.58 us
    ppermute x1, starting transfers between devices, early_half(): lax.ppermute(first, 'sp', [(i, quarter + (i + quarter // 2) % quarter) fo...  1.29 us
    pallas_call x1, Pallas kernels, per_device(): pl.pallas_call(functools.partial(norm_kernel, width * parts, total_length...  1.29 us
    ppermute x2, waiting for transfers between devices, after_first_quarter(): lax.ppermute(second, 'sp', pairs)  1.28 us
  transfers between devices with their start and end apart: 3, of which 1 were waited for; matrix products, arithmetic and copies ran while one was open for 0% of the time, Pallas kernels for 0%

profile of v7, /device:TPU:128, one launch (start us, length us, event | category | flops | bytes accessed | tf_op | source)
XLA Modules:
  0.0 40.6 jit_solution(12710190749697391000)
XLA Ops:
  0.0 2.6 %local.1 = (bf16[1024,512]{1,0:T(8,128)(2,1)S(1)}, f32[1024,512]{1,0:T(8,128)S(1)}, f32[8,8,128]{2,1,0:T(8,128)S(1)}, f32[8,128]{1,0:T(8,128)S(1)}) custom-call(f32[1024,512]{1,0:T(8,128)} %bitcast.5, bf16[1024,512]{1,0:T(8,128)(2,1)} %bitcast.6), custom_call_target="tpu_custom_call" | custom-call | tf_op jit(solution)/shard_map/local/pallas_call | solution.py:157
  2.7 0.0 copy-start
  2.7 24.0 %conditional.5 = (f32[8,128]{1,0:T(8,128)S(1)}, f32[8,128]{1,0:T(8,128)S(1)}) conditional(s32[]{:T(128)} %convert_element_type.14, f32[8,128]{1,0:T(8,128)S(1)} %get-tuple-element.61, (s32[]{:T(128)}, f32[8,128]{1,0:T(8,128)S(1)}) %tuple.39), branch_computations={%region_0.0_spmd, %region_1.0_spmd} | conditional | flops 4098 | bytes 446566 | solution.py:218
  2.7 1.3 %collective-permute-start = (f32[8,128]{1,0:T(8,128)S(1)}, f32[8,128]{1,0:T(8,128)S(1)}, u32[]{:S(2)}, u32[]{:S(2)}) collective-permute-start(f32[8,128]{1,0:T(8,128)S(1)} %get-tuple-element.38), channel_id=1, source_target_pairs={{0,192},{8,200},{16,208},{24,216},{32,224},{40,232},{48,240},{56,2... | collective-permute-start | bytes 12296 | tf_op jit(solution)/shard_map/cond/branch_1_fun/ppermute | solution.py:195
  4.0 22.6 %conditional.1 = ((f32[8,128]{1,0:T(8,128)S(1)}, f32[8,128]{1,0:T(8,128)S(1)}, f32[8,128]{1,0:T(8,128)S(1)}, f32[8,128]{1,0:T(8,128)S(1)})) conditional(s32[]{:T(128)} %convert_element_type.2, f32[8,128]{1,0:T(8,128)S(1)} %get-tuple-element.37, (f32[8,128]{1,0:T(8,128)S(1)}, f32[8,128]{1,0:T(8,128)S(1)}) %tuple.34), branch_computations={%region_4.0_spmd, %region_5.0_spmd} | conditional | bytes 200712 | solution.py:196
  4.1 22.5 %all_to_all.18.gathered = f32[16,8,128]{2,1,0:T(8,128)S(1)} all-to-all(f32[16,8,128]{2,1,0:T(8,128)S(1)} %broadcast_in_dim.11), channel_id=1, replica_groups={{0,8,16,24,32,40,48,56,64,72,80,88,96,104,112,120},{128,136,144,152,160..., dimensions={0} | all-to-all | bytes 131072 | tf_op jit(solution)/shard_map/cond/branch_1_fun/cond/branch_0_fun/all_to_all | solution.py:186
  26.6 0.0 collective-permute-done
  26.6 3.9 %conditional.6 = (f32[8,128]{1,0:T(8,128)S(1)}) conditional(s32[]{:T(128)} %convert_element_type.13, (f32[8,128]{1,0:T(8,128)S(1)}, s32[]{:T(128)}, f32[8,128]{1,0:T(8,128)S(1)}, f32[8,128]{1,0:T(8,128)S(1)}) %tuple.40, f32[8,128]{1,0:T(8,128)S(1)} %get-tuple-element.63), branch_computations={%region_6.0_spmd, %region_9.0_spmd} | conditional | flops 3074 | bytes 450686 | solution.py:219
  26.7 1.3 %collective-permute-start.2 = (f32[8,128]{1,0:T(8,128)S(1)}, f32[8,128]{1,0:T(8,128)S(1)}, u32[]{:S(2)}, u32[]{:S(2)}) collective-permute-start(f32[8,128]{1,0:T(8,128)S(1)} %get-tuple-element.44), channel_id=1, source_target_pairs={{128,448},{136,456},{144,464},{152,472},{160,480},{168,488},{176,4... | collective-permute-start | bytes 12296 | tf_op jit(solution)/shard_map/cond/branch_0_fun/ppermute | solution.py:207
  28.0 1.3 %collective-permute-start.1 = (f32[8,128]{1,0:T(8,128)S(1)}, f32[8,128]{1,0:T(8,128)S(1)}, u32[]{:S(2)}, u32[]{:S(2)}) collective-permute-start(f32[8,128]{1,0:T(8,128)S(1)} %get-tuple-element.44), channel_id=1, source_target_pairs={{128,320},{136,328},{144,336},{152,344},{160,352},{168,360},{176,3... | collective-permute-start | bytes 12296 | tf_op jit(solution)/shard_map/cond/branch_0_fun/ppermute | solution.py:207
  29.3 0.0 collective-permute-done.2
  29.3 1.3 %collective-permute-done.1 = f32[8,128]{1,0:T(8,128)S(1)} collective-permute-done((f32[8,128]{1,0:T(8,128)S(1)}, f32[8,128]{1,0:T(8,128)S(1)}, u32[]{:S(2)}, u32[]{:S(2)}) %collective-permute-start.1) | collective-permute-done | bytes 4128 | tf_op jit(solution)/shard_map/cond/branch_0_fun/ppermute | solution.py:207
  30.6 0.6 %carry.1 = (f32[1024,512]{1,0:T(8,128)S(1)}, f32[8,8,128]{2,1,0:T(8,128)S(1)}) custom-call(bf16[1024,512]{1,0:T(8,128)(2,1)S(1)} %get-tuple-element.58.drop, f32[1024,512]{1,0:T(8,128)S(1)} %get-tuple-element.59.inner, f32[8,8,128]{2,1,0:T(8,128)S(1)} %get-tuple-element.60.marks, f32[8,128]{1,0:T(8,128)S(1)} %get-tuple-element.91.start), custom_call_target="tpu_custom_call" | custom-call | tf_op jit(solution)/shard_map/carry/pallas_call | solution.py:223
  31.2 8.1 %all_to_all.20.powers = f32[8,8,128]{2,1,0:T(8,128)S(1)} all-to-all(f32[8,8,128]{2,1,0:T(8,128)S(1)} %get-tuple-element.65), channel_id=1, replica_groups=mesh['sp'=64,'tp'=8] {'tp'}, dimensions={0} | all-to-all | bytes 65536 | tf_op jit(solution)/shard_map/all_to_all | solution.py:231
  39.3 0.0 copy-done
  39.3 1.3 %norm.1 = bf16[1024,512]{1,0:T(8,128)(2,1)} custom-call(f32[1024,512]{1,0:T(8,128)S(1)} %get-tuple-element.64.forward, f32[8,8,128]{2,1,0:T(8,128)S(1)} %all_to_all.20.powers, f32[1,512]{1,0:T(1,128)S(1)} %bitcast.4), custom_call_target="tpu_custom_call" | custom-call | tf_op jit(solution)/shard_map/norm/pallas_call | solution.py:232
  (8 shorter events, 0.1 us)
Async XLA Ops:
  2.7 36.6 %copy-start = (f32[512]{0:T(512)S(1)}, f32[512]{0:T(512)}, u32[]{:S(2)}) copy-start(f32[512]{0:T(512)} %param.15) | copy-start | bytes 6148
  2.7 23.9 %collective-permute-start = (f32[8,128]{1,0:T(8,128)S(1)}, f32[8,128]{1,0:T(8,128)S(1)}, u32[]{:S(2)}, u32[]{:S(2)}) collective-permute-start(f32[8,128]{1,0:T(8,128)S(1)} %get-tuple-element.38), channel_id=1, source_target_pairs={{0,192},{8,200},{16,208},{24,216},{32,224},{40,232},{48,240},{56,2... | collective-permute-start | bytes 12296 | tf_op jit(solution)/shard_map/cond/branch_1_fun/ppermute | solution.py:195
  26.7 2.6 %collective-permute-start.2 = (f32[8,128]{1,0:T(8,128)S(1)}, f32[8,128]{1,0:T(8,128)S(1)}, u32[]{:S(2)}, u32[]{:S(2)}) collective-permute-start(f32[8,128]{1,0:T(8,128)S(1)} %get-tuple-element.44), channel_id=1, source_target_pairs={{128,448},{136,456},{144,464},{152,472},{160,480},{168,488},{176,4... | collective-permute-start | bytes 12296 | tf_op jit(solution)/shard_map/cond/branch_0_fun/ppermute | solution.py:207
  28.0 2.6 %collective-permute-start.1 = (f32[8,128]{1,0:T(8,128)S(1)}, f32[8,128]{1,0:T(8,128)S(1)}, u32[]{:S(2)}, u32[]{:S(2)}) collective-permute-start(f32[8,128]{1,0:T(8,128)S(1)} %get-tuple-element.44), channel_id=1, source_target_pairs={{128,320},{136,328},{144,336},{152,344},{160,352},{168,360},{176,3... | collective-permute-start | bytes 12296 | tf_op jit(solution)/shard_map/cond/branch_0_fun/ppermute | solution.py:207

commit v8 on v7

--- a/solution.py
+++ b/solution.py
@@ -133,8 +133,10 @@
     for s in range(length // lanes):
         rows = pl.ds(s * lanes, lanes)
         staged[rows, :] = (forward[rows, :] * scale[:, s : s + 1] * gain[...]).astype(BF16)
-        copies.append(pltpu.make_async_copy(staged.at[rows], out.at[rows], sems.at[s]))
-        copies[-1].start()
+        if s % 2:
+            pair = pl.ds((s - 1) * lanes, 2 * lanes)
+            copies.append(pltpu.make_async_copy(staged.at[pair], out.at[pair], sems.at[s // 2]))
+            copies[-1].start()
     for copy in copies:
         copy.wait()
 
@@ -236,7 +238,7 @@
         out_specs=HBM,
         scratch_shapes=[
             pltpu.VMEM((length, width), BF16),
-            pltpu.SemaphoreType.DMA((length // LANES,)),
+            pltpu.SemaphoreType.DMA((length // LANES // 2,)),
         ],
         compiler_params=limit,
         name="norm",

time: 40.8 us -> 40.8 us (level)
  no operation moved by 1% of the time
where the time goes in v8:
time: 40.8 us; the launch traced here: 40.6 us
  blocking collectives  30.6 us (75%)
  Pallas kernels  4.53 us (11%)
  starting transfers between devices  3.87 us (9%)
  waiting for transfers between devices  1.28 us (3%)
    all_to_all x1, blocking collectives, found(): lax.all_to_all(copies, 'sp', 0, 0, axis_index_groups=groups, tiled=True)  22.5 us
    all_to_all x1, blocking collectives, per_device(): powers = lax.all_to_all(power, 'tp', 0, 0, tiled=True)  8.12 us
    pallas_call x1, Pallas kernels, per_device(): pl.pallas_call(functools.partial(local_kernel, block, stages, rate), out_...  2.64 us
    ppermute x2, starting transfers between devices, after_first_quarter(): lax.ppermute(second, 'sp', pairs)  2.58 us
    ppermute x1, starting transfers between devices, early_half(): lax.ppermute(first, 'sp', [(i, quarter + (i + quarter // 2) % quarter) fo...  1.29 us
    ppermute x2, waiting for transfers between devices, after_first_quarter(): lax.ppermute(second, 'sp', pairs)  1.28 us
    pallas_call x1, Pallas kernels, per_device(): pl.pallas_call(functools.partial(norm_kernel, width * parts, total_length...  1.26 us
  transfers between devices with their start and end apart: 3, of which 1 were waited for; matrix products, arithmetic and copies ran while one was open for 0% of the time, Pallas kernels for 0%

profile of v8, /device:TPU:128, one launch (start us, length us, event | category | flops | bytes accessed | tf_op | source)
XLA Modules:
  0.0 40.6 jit_solution(10323720757047159124)
XLA Ops:
  0.0 2.6 %local.1 = (bf16[1024,512]{1,0:T(8,128)(2,1)S(1)}, f32[1024,512]{1,0:T(8,128)S(1)}, f32[8,8,128]{2,1,0:T(8,128)S(1)}, f32[8,128]{1,0:T(8,128)S(1)}) custom-call(f32[1024,512]{1,0:T(8,128)} %bitcast.5, bf16[1024,512]{1,0:T(8,128)(2,1)} %bitcast.6), custom_call_target="tpu_custom_call" | custom-call | tf_op jit(solution)/shard_map/local/pallas_call | solution.py:159
  2.7 0.0 copy-start
  2.7 24.0 %conditional.5 = (f32[8,128]{1,0:T(8,128)S(1)}, f32[8,128]{1,0:T(8,128)S(1)}) conditional(s32[]{:T(128)} %convert_element_type.14, f32[8,128]{1,0:T(8,128)S(1)} %get-tuple-element.61, (s32[]{:T(128)}, f32[8,128]{1,0:T(8,128)S(1)}) %tuple.39), branch_computations={%region_0.0_spmd, %region_1.0_spmd} | conditional | flops 4098 | bytes 446566 | solution.py:220
  2.7 1.3 %collective-permute-start = (f32[8,128]{1,0:T(8,128)S(1)}, f32[8,128]{1,0:T(8,128)S(1)}, u32[]{:S(2)}, u32[]{:S(2)}) collective-permute-start(f32[8,128]{1,0:T(8,128)S(1)} %get-tuple-element.38), channel_id=1, source_target_pairs={{0,192},{8,200},{16,208},{24,216},{32,224},{40,232},{48,240},{56,2... | collective-permute-start | bytes 12296 | tf_op jit(solution)/shard_map/cond/branch_1_fun/ppermute | solution.py:197
  4.0 22.6 %conditional.1 = ((f32[8,128]{1,0:T(8,128)S(1)}, f32[8,128]{1,0:T(8,128)S(1)}, f32[8,128]{1,0:T(8,128)S(1)}, f32[8,128]{1,0:T(8,128)S(1)})) conditional(s32[]{:T(128)} %convert_element_type.2, f32[8,128]{1,0:T(8,128)S(1)} %get-tuple-element.37, (f32[8,128]{1,0:T(8,128)S(1)}, f32[8,128]{1,0:T(8,128)S(1)}) %tuple.34), branch_computations={%region_4.0_spmd, %region_5.0_spmd} | conditional | bytes 200712 | solution.py:198
  4.1 22.5 %all_to_all.18.gathered = f32[16,8,128]{2,1,0:T(8,128)S(1)} all-to-all(f32[16,8,128]{2,1,0:T(8,128)S(1)} %broadcast_in_dim.11), channel_id=1, replica_groups={{0,8,16,24,32,40,48,56,64,72,80,88,96,104,112,120},{128,136,144,152,160..., dimensions={0} | all-to-all | bytes 131072 | tf_op jit(solution)/shard_map/cond/branch_1_fun/cond/branch_0_fun/all_to_all | solution.py:188
  26.6 0.0 collective-permute-done
  26.6 3.9 %conditional.6 = (f32[8,128]{1,0:T(8,128)S(1)}) conditional(s32[]{:T(128)} %convert_element_type.13, (f32[8,128]{1,0:T(8,128)S(1)}, s32[]{:T(128)}, f32[8,128]{1,0:T(8,128)S(1)}, f32[8,128]{1,0:T(8,128)S(1)}) %tuple.40, f32[8,128]{1,0:T(8,128)S(1)} %get-tuple-element.63), branch_computations={%region_6.0_spmd, %region_9.0_spmd} | conditional | flops 3074 | bytes 450686 | solution.py:221
  26.7 1.3 %collective-permute-start.2 = (f32[8,128]{1,0:T(8,128)S(1)}, f32[8,128]{1,0:T(8,128)S(1)}, u32[]{:S(2)}, u32[]{:S(2)}) collective-permute-start(f32[8,128]{1,0:T(8,128)S(1)} %get-tuple-element.44), channel_id=1, source_target_pairs={{128,448},{136,456},{144,464},{152,472},{160,480},{168,488},{176,4... | collective-permute-start | bytes 12296 | tf_op jit(solution)/shard_map/cond/branch_0_fun/ppermute | solution.py:209
  28.0 1.3 %collective-permute-start.1 = (f32[8,128]{1,0:T(8,128)S(1)}, f32[8,128]{1,0:T(8,128)S(1)}, u32[]{:S(2)}, u32[]{:S(2)}) collective-permute-start(f32[8,128]{1,0:T(8,128)S(1)} %get-tuple-element.44), channel_id=1, source_target_pairs={{128,320},{136,328},{144,336},{152,344},{160,352},{168,360},{176,3... | collective-permute-start | bytes 12296 | tf_op jit(solution)/shard_map/cond/branch_0_fun/ppermute | solution.py:209
  29.3 0.0 collective-permute-done.2
  29.3 1.3 %collective-permute-done.1 = f32[8,128]{1,0:T(8,128)S(1)} collective-permute-done((f32[8,128]{1,0:T(8,128)S(1)}, f32[8,128]{1,0:T(8,128)S(1)}, u32[]{:S(2)}, u32[]{:S(2)}) %collective-permute-start.1) | collective-permute-done | bytes 4128 | tf_op jit(solution)/shard_map/cond/branch_0_fun/ppermute | solution.py:209
  30.6 0.6 %carry.1 = (f32[1024,512]{1,0:T(8,128)S(1)}, f32[8,8,128]{2,1,0:T(8,128)S(1)}) custom-call(bf16[1024,512]{1,0:T(8,128)(2,1)S(1)} %get-tuple-element.58.drop, f32[1024,512]{1,0:T(8,128)S(1)} %get-tuple-element.59.inner, f32[8,8,128]{2,1,0:T(8,128)S(1)} %get-tuple-element.60.marks, f32[8,128]{1,0:T(8,128)S(1)} %get-tuple-element.91.start), custom_call_target="tpu_custom_call" | custom-call | tf_op jit(solution)/shard_map/carry/pallas_call | solution.py:225
  31.2 8.1 %all_to_all.20.powers = f32[8,8,128]{2,1,0:T(8,128)S(1)} all-to-all(f32[8,8,128]{2,1,0:T(8,128)S(1)} %get-tuple-element.65), channel_id=1, replica_groups=mesh['sp'=64,'tp'=8] {'tp'}, dimensions={0} | all-to-all | bytes 65536 | tf_op jit(solution)/shard_map/all_to_all | solution.py:233
  39.3 0.0 copy-done
  39.3 1.3 %norm.1 = bf16[1024,512]{1,0:T(8,128)(2,1)} custom-call(f32[1024,512]{1,0:T(8,128)S(1)} %get-tuple-element.64.forward, f32[8,8,128]{2,1,0:T(8,128)S(1)} %all_to_all.20.powers, f32[1,512]{1,0:T(1,128)S(1)} %bitcast.4), custom_call_target="tpu_custom_call" | custom-call | tf_op jit(solution)/shard_map/norm/pallas_call | solution.py:234
  (8 shorter events, 0.1 us)
Async XLA Ops:
  2.7 36.6 %copy-start = (f32[512]{0:T(512)S(1)}, f32[512]{0:T(512)}, u32[]{:S(2)}) copy-start(f32[512]{0:T(512)} %param.15) | copy-start | bytes 6148
  2.7 23.9 %collective-permute-start = (f32[8,128]{1,0:T(8,128)S(1)}, f32[8,128]{1,0:T(8,128)S(1)}, u32[]{:S(2)}, u32[]{:S(2)}) collective-permute-start(f32[8,128]{1,0:T(8,128)S(1)} %get-tuple-element.38), channel_id=1, source_target_pairs={{0,192},{8,200},{16,208},{24,216},{32,224},{40,232},{48,240},{56,2... | collective-permute-start | bytes 12296 | tf_op jit(solution)/shard_map/cond/branch_1_fun/ppermute | solution.py:197
  26.7 2.6 %collective-permute-start.2 = (f32[8,128]{1,0:T(8,128)S(1)}, f32[8,128]{1,0:T(8,128)S(1)}, u32[]{:S(2)}, u32[]{:S(2)}) collective-permute-start(f32[8,128]{1,0:T(8,128)S(1)} %get-tuple-element.44), channel_id=1, source_target_pairs={{128,448},{136,456},{144,464},{152,472},{160,480},{168,488},{176,4... | collective-permute-start | bytes 12296 | tf_op jit(solution)/shard_map/cond/branch_0_fun/ppermute | solution.py:209
  28.0 2.6 %collective-permute-start.1 = (f32[8,128]{1,0:T(8,128)S(1)}, f32[8,128]{1,0:T(8,128)S(1)}, u32[]{:S(2)}, u32[]{:S(2)}) collective-permute-start(f32[8,128]{1,0:T(8,128)S(1)} %get-tuple-element.44), channel_id=1, source_target_pairs={{128,320},{136,328},{144,336},{152,344},{160,352},{168,360},{176,3... | collective-permute-start | bytes 12296 | tf_op jit(solution)/shard_map/cond/branch_0_fun/ppermute | solution.py:209
